TPU v7x, 512 devices: a whole 4x8x8 slice. The times are simulated.
512 devices in a mesh: group: 16 (over z, core), tensor: 32 (over y, x).
Axes of the slice: x: 4, y: 8, z: 8, core: 2. Of those that a mesh axis runs over, the one named last changes fastest.
Arguments:
- key_value_cache: bfloat16 [1024, 1024, 256], P(('group', 'tensor')), may hold values from -8 to 8
- queries: bfloat16 [128, 48, 128], P('group'), may hold values from -200 to 200
- fresh_key_value: bfloat16 [128, 8, 256], P('group'), may hold values from -6 to 6
- lengths: int32 [128], P('group'), may hold values from 2 to 1023
- residual: bfloat16 [128, 6144], P('group'), may hold values from -100 to 100
- norm_gain: float32 [6144], replicated, may hold values from 0.1 to 1.9
- router_weight: bfloat16 [6144, 8], replicated, may hold values from -0.078125 to 0.078125
- routing: int32 [128, 2], P('group'), may hold values from 0 to 7, all different within a row
- expert_gate: bfloat16 [8, 6144, 8192], P(None, 'group', 'tensor'), may hold values from -0.078125 to 0.078125
- expert_up: bfloat16 [8, 6144, 8192], P(None, 'group', 'tensor'), may hold values from -0.078125 to 0.078125
Outputs:
- updated: bfloat16 [128, 6144], P('group')
- expert_hidden: bfloat16 [128, 2, 8192], P('group', None, 'tensor')
- new_cache: bfloat16 [128, 8, 1024, 256], P('group', None, 'tensor')
Inputs may be any that keep to these rules, and one draw needn't show every extreme that they name: Slot lengths[s] of sequence s receives its new token. `routing`: A token's two experts differ.
All inputs are finite; a program needn't handle non-finite values.
Results may differ from a plain program's by a relative error of at most 0.028.
Values may be sent and summed in bfloat16 or wider, within the bound.
A program may use at most 64 MiB of HBM per device.

v0:
```python
import math

import jax
import jax.numpy as jnp
from jax import lax
from jax.sharding import PartitionSpec as P


def from_everyone(value, axis):
    size = lax.axis_size(axis)
    return lax.all_to_all(
        jnp.broadcast_to(value[None], (size, *value.shape)), axis, 0, 0, tiled=True
    )


def in_order(parts, dim):
    parts = jnp.moveaxis(parts, 0, dim)
    lengths = parts.shape
    return parts.reshape(*lengths[:dim], lengths[dim] * lengths[dim + 1], *lengths[dim + 2 :])


def collect(value, axis, dim):
    parts = from_everyone(value, axis)
    return in_order(parts, dim)


def cut_along(value, dim, size):
    before, after = (value.shape[:dim], value.shape[dim + 1 :])
    return jnp.moveaxis(value.reshape(*before, size, -1, *after), dim, 0)


def summed_on_arrival(value, axis, dim):
    size = lax.axis_size(axis)
    parts = lax.all_to_all(cut_along(value, dim, size), axis, 0, 0, tiled=True)
    return jnp.sum(parts.astype(jnp.float32), axis=0)


def body(
    key_value_cache,
    queries,
    fresh_key_value,
    lengths,
    residual,
    norm_gain,
    router_weight,
    routing,
    expert_gate,
    expert_up,
):
    tensor_rank = lax.axis_index("tensor")
    seq_local = queries.shape[0]
    q_heads = queries.shape[1]
    kv_heads = fresh_key_value.shape[1]
    head_size = fresh_key_value.shape[2] // 2
    query_group_width = q_heads // kv_heads
    score_scale = 1.0 / math.sqrt(head_size)
    arrived = lax.all_to_all(key_value_cache, "tensor", split_axis=1, concat_axis=0, tiled=True)
    local_span = arrived.shape[1]
    arrived = arrived.reshape(seq_local, kv_heads, local_span, 2 * head_size)
    slot_index = tensor_rank * local_span + lax.broadcasted_iota(jnp.int32, (local_span,), 0)
    new_slot = slot_index[None, None, :, None] == lengths[:, None, None, None]
    new_cache = jnp.where(new_slot, fresh_key_value[:, :, None, :], arrived)
    pair_count = key_value_cache.shape[0]
    pair_begin = tensor_rank * pair_count
    query_vectors = lax.dynamic_slice_in_dim(
        queries.reshape(seq_local * kv_heads, query_group_width, head_size),
        pair_begin,
        pair_count,
        0,
    )
    own_rows = lax.dynamic_slice_in_dim(
        fresh_key_value.reshape(seq_local * kv_heads, 2 * head_size), pair_begin, pair_count, 0
    )
    every_length = jnp.broadcast_to(lengths[:, None], (seq_local, kv_heads)).reshape(
        seq_local * kv_heads
    )
    pair_length = lax.dynamic_slice_in_dim(every_length, pair_begin, pair_count, 0)
    scores = (
        jnp.einsum(
            "pgd,ptd->pgt",
            query_vectors,
            key_value_cache[..., :head_size],
            preferred_element_type=jnp.float32,
        )
        * score_scale
    )
    own_score = (
        jnp.einsum(
            "pgd,pd->pg", query_vectors, own_rows[:, :head_size], preferred_element_type=jnp.float32
        )
        * score_scale
    )
    visible = (
        lax.broadcasted_iota(jnp.int32, (1, 1, key_value_cache.shape[1]), 2)
        < pair_length[:, None, None]
    )
    peak = jnp.maximum(jnp.max(jnp.where(visible, scores, -1e30), -1), own_score)
    attention_weights = jnp.where(visible, jnp.exp(scores - peak[..., None]), 0.0)
    own_weight = jnp.exp(own_score - peak)
    denominator = jnp.sum(attention_weights, -1) + own_weight
    weighted = jnp.einsum(
        "pgt,ptd->pgd",
        attention_weights.astype(jnp.bfloat16),
        key_value_cache[..., head_size:],
        preferred_element_type=jnp.float32,
    )
    own_rounded = lax.optimization_barrier(own_weight.astype(jnp.bfloat16)).astype(jnp.float32)
    weighted = weighted + own_rounded[..., None] * own_rows[:, None, head_size:].astype(jnp.float32)
    head_result = (weighted / denominator[..., None]).reshape(
        pair_count, query_group_width * head_size
    )
    gathered = collect(head_result, "tensor", 0)
    attention = gathered.reshape(seq_local, q_heads * head_size)
    updated = (residual.astype(jnp.float32) + attention).astype(jnp.bfloat16)
    stream = updated.astype(jnp.float32)
    normed = (
        stream * lax.rsqrt(jnp.mean(stream * stream, -1, keepdims=True) + 1e-05) * norm_gain
    ).astype(jnp.bfloat16)
    logits = jnp.dot(normed, router_weight, preferred_element_type=jnp.float32)
    expert_count = router_weight.shape[1]
    expert_ids = lax.broadcasted_iota(jnp.int32, (1, 1, expert_count), 2)
    chosen_mask = routing[:, :, None] == expert_ids
    chosen_logits = jnp.sum(jnp.where(chosen_mask, logits[:, None, :], 0.0), -1)
    gate_weights = jax.nn.sigmoid(chosen_logits - chosen_logits[:, ::-1])
    columns = lax.all_to_all(normed, "group", split_axis=1, concat_axis=0, tiled=True)
    every_route = collect(routing, "group", 0)
    gate_part = jnp.einsum("td,edf->tef", columns, expert_gate, preferred_element_type=jnp.float32)
    up_part = jnp.einsum("td,edf->tef", columns, expert_up, preferred_element_type=jnp.float32)
    products_term = jnp.stack((gate_part, up_part), 2)
    route_mask = every_route[:, :, None] == expert_ids
    picked = summed_on_arrival(
        jnp.sum(jnp.where(route_mask[:, :, :, None, None], products_term[:, None], 0.0), 2).astype(
            jnp.bfloat16
        ),
        "group",
        0,
    )
    expert_hidden = (
        gate_weights[:, :, None] * jax.nn.silu(picked[:, :, 0]) * picked[:, :, 1]
    ).astype(jnp.bfloat16)
    return (updated, expert_hidden, new_cache)


def solution(mesh):
    in_specs = (
        P(("group", "tensor"), None, None),
        P("group", None, None),
        P("group", None, None),
        P("group"),
        P("group", None),
        P(),
        P(),
        P("group", None),
        P(None, "group", "tensor"),
        P(None, "group", "tensor"),
    )
    out_specs = (P("group", None), P("group", None, "tensor"), P("group", None, "tensor", None))
    return jax.shard_map(body, mesh=mesh, in_specs=in_specs, out_specs=out_specs, check_vma=False)
```

profile of v0, /device:TPU:1, one launch (start us, length us, event | category | flops | bytes accessed | tf_op | source)
XLA Modules:
  0.0 114.3 jit_solution(13200046791733191354)
XLA Ops:
  0.6 0.0 copy-start
  0.6 1.4 %broadcast_in_dim.108 = s32[16,8,2]{1,2,0:T(2,128)} broadcast(s32[8,2]{0,1:T(2,128)} %param.17), dimensions={1,2} | broadcast | bytes 1088 | tf_op jit(solution)/shard_map/broadcast_in_dim | solution.py:12
  2.1 11.8 %all-to-all-start.1 = ((s32[16,8,2]{1,2,0:T(2,128)}), s32[16,8,2]{1,2,0:T(2,128)S(1)}, u32[]{:S(2)}, u32[]{:S(2)}) async-start(s32[16,8,2]{1,2,0:T(2,128)} %broadcast_in_dim.108), calls=%async_computation.1 | async-start | bytes 32768 | tf_op jit(solution)/shard_map/all_to_all | solution.py:11
  13.9 0.7 broadcast_in_dim.100
  14.6 0.1 reshape.108
  14.7 0.1 dynamic_slice.9
  14.8 0.1 iota_compare_fusion.2
  14.8 0.9 reshape.109
  15.8 0.8 dynamic-slice_convert_fusion
  16.5 0.1 fusion.17
  16.7 1.4 %select_reduce_fusion.1 = (f32[2,6]{1,0:T(2,128)S(1)}, f32[2,6,1024]{2,1,0:T(8,128)S(1)}) fusion(pred[2,1024]{1,0:T(4,128)(4,1)S(1)} %iota_compare_fusion.2, bf16[2,1024,256]{2,1,0:T(8,128)(2,1)} %param.10, bf16[64,6,128]{2,1,0:T(8,128)(2,1)S(1)} %reshape.109, s32[]{:T(128)S(6)} %select_n.24), kind=kOutput, calls=%fused_computation.22 | convolution fusion | flops 3182580 | bytes 581684 | tf_op jit(solution)/shard_map/pgd,ptd->pgt/dot_general | solution.py:79
  18.0 0.2 fusion.9
  18.2 1.3 %fusion.1 = f32[1,2,6,128]{3,2,1,0:T(8,128)S(1)} fusion(bf16[2,1024,256]{2,1,0:T(8,128)(2,1)} %param.10, f32[2,6,1024]{2,1,0:T(8,128)S(1)} %get-tuple-element.13, f32[2,6]{1,0:T(2,128)S(1)} %multiply_maximum_fusion, pred[2,1024]{1,0:T(4,128)(4,1)S(1)} %iota_compare_fusion.2, f32[2,6]{1,0:T(2,128)S(1)} %get-tuple-element.11, ...), kind=kOutput, calls=%fused_computation.7 | convolution fusion | flops 3187200 | bytes 582800 | tf_op jit(solution)/shard_map/pgt,ptd->pgd/dot_general | solution.py:101
  19.5 1.7 %all-to-all-done.1 = s32[16,8,2]{1,2,0:T(2,128)S(1)} async-done(((s32[16,8,2]{1,2,0:T(2,128)}), s32[16,8,2]{1,2,0:T(2,128)S(1)}, u32[]{:S(2)}, u32[]{:S(2)}) %all-to-all-start.1) | async-done | bytes 1056 | tf_op jit(solution)/shard_map/all_to_all | solution.py:11
  21.2 0.7 broadcast_in_dim.105
  21.9 9.7 %all-to-all-start = ((f32[32,2,768]{2,1,0:T(2,128)}), f32[32,2,768]{2,1,0:T(2,128)S(1)}, u32[]{:S(2)}, u32[]{:S(2)}) async-start(f32[32,2,768]{2,1,0:T(2,128)} %broadcast_in_dim.105), calls=%async_computation | async-start | bytes 393216 | tf_op jit(solution)/shard_map/all_to_all | solution.py:11
  31.6 0.0 copy-start.2
  31.6 0.8 copy.41
  32.4 9.8 %all-to-all-done = f32[32,2,768]{2,1,0:T(2,128)S(1)} async-done(((f32[32,2,768]{2,1,0:T(2,128)}), f32[32,2,768]{2,1,0:T(2,128)S(1)}, u32[]{:S(2)}, u32[]{:S(2)}) %all-to-all-start) | async-done | bytes 196640 | tf_op jit(solution)/shard_map/all_to_all | solution.py:11
  42.2 0.2 reshape_reshape.3
  42.4 1.1 fusion.4
  43.4 1.5 %fusion.6 = bf16[8,6144]{1,0:T(8,128)(2,1)} fusion(bf16[8,6144]{1,0:T(8,128)(2,1)S(1)} %get-tuple-element.7, f32[6144]{0:T(1024)} %param.15, f32[8]{0:T(128)S(1)} %add_rsqrt_fusion), kind=kLoop, calls=%fused_computation.16 | loop fusion | flops 196608 | bytes 221216 | tf_op jit(solution)/shard_map/convert_element_type | solution.py:118
  45.0 7.1 %all-to-all-start.2 = ((bf16[8,16,384]{2,0,1:T(8,128)(2,1)}), bf16[8,16,384]{2,0,1:T(8,128)(2,1)S(1)}, u32[]{:S(2)}, u32[]{:S(2)}) async-start(bf16[8,16,384]{2,0,1:T(8,128)(2,1)} %bitcast.5), calls=%async_computation.2 | async-start | bytes 196608 | tf_op jit(solution)/shard_map/all_to_all | solution.py:125
  52.1 1.0 iota_compare_fusion
  53.1 7.4 %all-to-all-done.2 = bf16[8,16,384]{2,0,1:T(8,128)(2,1)S(1)} async-done(((bf16[8,16,384]{2,0,1:T(8,128)(2,1)}), bf16[8,16,384]{2,0,1:T(8,128)(2,1)S(1)}, u32[]{:S(2)}, u32[]{:S(2)}) %all-to-all-start.2) | async-done | bytes 98336 | tf_op jit(solution)/shard_map/all_to_all | solution.py:125
  60.5 0.4 convolution_bitcast_fusion
  61.0 0.4 convolution_bitcast_fusion.1
  61.4 0.2 pad_maximum_fusion
  61.6 1.2 %copy.33 = f32[128,8,2,256]{3,1,2,0:T(8,128)S(1)} copy(f32[128,8,2,256]{3,0,1,2:T(8,128)S(1)} %pad_maximum_fusion) | data formatting | bytes 4194304 | tf_op jit(solution)/shard_map/stack | solution.py:129
  62.8 0.0 copy-start.1
  62.9 1.7 %select_reduce_fusion = bf16[128,2,2,256]{3,2,1,0:T(2,128)(2,1)S(1)} fusion(f32[128,8,2,256]{3,1,2,0:T(8,128)S(1)} %copy.33, pred[128,2,8]{2,1,0:T(4,128)(4,1)S(1)} %iota_compare_fusion), kind=kLoop, calls=%fused_computation | loop fusion | flops 1966080 | bytes 2361344 | tf_op jit(solution)/shard_map/reduce_sum | solution.py:132
  64.6 0.7 copy.34
  65.3 3.4 %all-to-all-start.3 = ((bf16[16,8,2,2,256]{4,1,3,2,0:T(8,128)(2,1)}), bf16[16,8,2,2,256]{4,1,3,2,0:T(8,128)(2,1)S(1)}, u32[]{:S(2)}, u32[]{:S(2)}) async-start(bf16[16,8,2,2,256]{4,1,3,2,0:T(8,128)(2,1)} %copy.34), calls=%async_computation.3 | async-start | bytes 524288 | tf_op jit(solution)/shard_map/all_to_all | solution.py:34
  68.7 0.0 copy-start.7
  68.8 0.0 copy-start.4
  68.8 0.0 copy-start.6
  68.8 2.0 %copy.36 = bf16[2,1024,256]{2,0,1:T(2,128)(2,1)} copy(bf16[2,1024,256]{2,1,0:T(8,128)(2,1)S(1)} %copy-done.1) | data formatting | bytes 2097152 | tf_op args[0]
  70.8 9.6 %all-to-all-done.3 = bf16[16,8,2,2,256]{4,1,3,2,0:T(8,128)(2,1)S(1)} async-done(((bf16[16,8,2,2,256]{4,1,3,2,0:T(8,128)(2,1)}), bf16[16,8,2,2,256]{4,1,3,2,0:T(8,128)(2,1)S(1)}, u32[]{:S(2)}, u32[]{:S(2)}) %all-to-all-start.3) | async-done | bytes 262176 | tf_op jit(solution)/shard_map/all_to_all | solution.py:34
  80.5 3.9 %all-to-all-start.4 = ((bf16[2,1024,256]{2,0,1:T(2,128)(2,1)}), bf16[2,1024,256]{2,0,1:T(2,128)(2,1)S(1)}, u32[]{:S(2)}, u32[]{:S(2)}) async-start(bf16[2,1024,256]{2,0,1:T(2,128)(2,1)} %copy.36), calls=%async_computation.4 | async-start | bytes 2097152 | tf_op jit(solution)/shard_map/all_to_all | solution.py:57
  84.4 0.1 broadcast_compare_fusion
  84.5 1.1 fusion.26
  85.6 0.2 select_reduce_fusion.2
  85.8 0.1 convert_reduce_fusion
  85.8 0.1 fusion.16
  85.9 0.6 copy.38
  86.5 26.4 %all-to-all-done.4 = bf16[2,1024,256]{2,0,1:T(2,128)(2,1)S(1)} async-done(((bf16[2,1024,256]{2,0,1:T(2,128)(2,1)}), bf16[2,1024,256]{2,0,1:T(2,128)(2,1)S(1)}, u32[]{:S(2)}, u32[]{:S(2)}) %all-to-all-start.4) | async-done | bytes 1048608 | tf_op jit(solution)/shard_map/all_to_all | solution.py:57
  112.9 0.2 copy.37
  113.1 1.1 bitcast_select_fusion
  (18 shorter events, 0.1 us)
Async XLA Ops:
  0.6 59.9 %copy-start = (bf16[8,384,256]{2,1,0:T(8,128)(2,1)S(1)}, bf16[8,384,256]{2,1,0:T(8,128)(2,1)}, u32[]{:S(2)}) copy-start(bf16[8,384,256]{2,1,0:T(8,128)(2,1)} %param.19) | copy-start | bytes 4718596
  2.1 19.2 %all-to-all-start.1 = ((s32[16,8,2]{1,2,0:T(2,128)}), s32[16,8,2]{1,2,0:T(2,128)S(1)}, u32[]{:S(2)}, u32[]{:S(2)}) async-start(s32[16,8,2]{1,2,0:T(2,128)} %broadcast_in_dim.108), calls=%async_computation.1 | async-start | bytes 32768 | tf_op jit(solution)/shard_map/all_to_all | solution.py:11
  21.9 20.3 %all-to-all-start = ((f32[32,2,768]{2,1,0:T(2,128)}), f32[32,2,768]{2,1,0:T(2,128)S(1)}, u32[]{:S(2)}, u32[]{:S(2)}) async-start(f32[32,2,768]{2,1,0:T(2,128)} %broadcast_in_dim.105), calls=%async_computation | async-start | bytes 393216 | tf_op jit(solution)/shard_map/all_to_all | solution.py:11
  31.6 29.4 %copy-start.2 = (bf16[8,384,256]{2,1,0:T(8,128)(2,1)S(1)}, bf16[8,384,256]{2,1,0:T(8,128)(2,1)}, u32[]{:S(2)}) copy-start(bf16[8,384,256]{2,1,0:T(8,128)(2,1)} %param.18) | copy-start | bytes 4718596
  43.4 18.0 %copy-start.3 = (bf16[8,6144]{1,0:T(8,128)(2,1)}, bf16[8,6144]{1,0:T(8,128)(2,1)S(1)}, u32[]{:S(2)}) copy-start(bf16[8,6144]{1,0:T(8,128)(2,1)S(1)} %get-tuple-element.7) | copy-start | bytes 294916
  45.0 15.6 %all-to-all-start.2 = ((bf16[8,16,384]{2,0,1:T(8,128)(2,1)}), bf16[8,16,384]{2,0,1:T(8,128)(2,1)S(1)}, u32[]{:S(2)}, u32[]{:S(2)}) async-start(bf16[8,16,384]{2,0,1:T(8,128)(2,1)} %bitcast.5), calls=%async_computation.2 | async-start | bytes 196608 | tf_op jit(solution)/shard_map/all_to_all | solution.py:125
  62.8 5.9 %copy-start.1 = (bf16[2,1024,256]{2,1,0:T(8,128)(2,1)S(1)}, bf16[2,1024,256]{2,1,0:T(8,128)(2,1)}, u32[]{:S(2)}) copy-start(bf16[2,1024,256]{2,1,0:T(8,128)(2,1)} %param.10) | copy-start | bytes 3145732
  65.3 15.2 %all-to-all-start.3 = ((bf16[16,8,2,2,256]{4,1,3,2,0:T(8,128)(2,1)}), bf16[16,8,2,2,256]{4,1,3,2,0:T(8,128)(2,1)S(1)}, u32[]{:S(2)}, u32[]{:S(2)}) async-start(bf16[16,8,2,2,256]{4,1,3,2,0:T(8,128)(2,1)} %copy.34), calls=%async_computation.3 | async-start | bytes 524288 | tf_op jit(solution)/shard_map/all_to_all | solution.py:34
  68.7 15.7 %copy-start.7 = (s32[8]{0:T(128)S(1)}, s32[8]{0:T(128)}, u32[]{:S(2)}) copy-start(s32[8]{0:T(128)} %param.13) | copy-start | bytes 100
  68.8 15.8 %copy-start.4 = (bf16[6144,8]{0,1:T(8,128)(2,1)S(1)}, bf16[6144,8]{0,1:T(8,128)(2,1)}, u32[]{:S(2)}) copy-start(bf16[6144,8]{0,1:T(8,128)(2,1)} %param.16) | copy-start | bytes 294916
  68.8 16.8 %copy-start.6 = (s32[8,2]{0,1:T(2,128)S(1)}, s32[8,2]{0,1:T(2,128)}, u32[]{:S(2)}) copy-start(s32[8,2]{0,1:T(2,128)} %param.17) | copy-start | bytes 196
  70.8 42.3 %copy-start.5 = (bf16[8,8,256]{2,1,0:T(8,128)(2,1)S(1)}, bf16[8,8,256]{2,1,0:T(8,128)(2,1)}, u32[]{:S(2)}) copy-start(bf16[8,8,256]{2,1,0:T(8,128)(2,1)} %param.12) | copy-start | bytes 98308
  80.5 32.4 %all-to-all-start.4 = ((bf16[2,1024,256]{2,0,1:T(2,128)(2,1)}), bf16[2,1024,256]{2,0,1:T(2,128)(2,1)S(1)}, u32[]{:S(2)}, u32[]{:S(2)}) async-start(bf16[2,1024,256]{2,0,1:T(2,128)(2,1)} %copy.36), calls=%async_computation.4 | async-start | bytes 2097152 | tf_op jit(solution)/shard_map/all_to_all | solution.py:57
where the time goes:
time: 115 us; the launch traced here: 114 us
  waiting for transfers between devices  54.9 us (48%)
  starting transfers between devices  36 us (31%)
  local copies, waits for them, and re-layouts  9.79 us (9%)
  other arithmetic  8.06 us (7%)
  matrix products  4.69 us (4%)
    all_to_all x1, waiting for transfers between devices, body(): lax.all_to_all(key_value_cache, 'tensor', split_axis=1, concat_axis=0, ti...  26.4 us
    all_to_all x2, starting transfers between devices, from_everyone(): lax.all_to_all(jnp.broadcast_to(value[None], (size, *value.shape)), axis,...  21.5 us
    all_to_all x2, waiting for transfers between devices, from_everyone(): lax.all_to_all(jnp.broadcast_to(value[None], (size, *value.shape)), axis,...  11.5 us
    all_to_all x1, waiting for transfers between devices, summed_on_arrival(): parts = lax.all_to_all(cut_along(value, dim, size), axis, 0, 0, tiled=True)  9.65 us
    all_to_all x1, waiting for transfers between devices, body(): lax.all_to_all(normed, 'group', split_axis=1, concat_axis=0, tiled=True)  7.41 us
    all_to_all x1, starting transfers between devices, body(): lax.all_to_all(normed, 'group', split_axis=1, concat_axis=0, tiled=True)  7.12 us
    all_to_all x1, starting transfers between devices, body(): lax.all_to_all(key_value_cache, 'tensor', split_axis=1, concat_axis=0, ti...  3.93 us
    all_to_all x1, starting transfers between devices, summed_on_arrival(): parts = lax.all_to_all(cut_along(value, dim, size), axis, 0, 0, tiled=True)  3.43 us
  transfers between devices with their start and end apart: 5, of which 5 were waited for; matrix products, arithmetic and copies ran while one was open for 10% of the time, Pallas kernels for 0%

commit v1 on v0

v1 whole, which is shorter than its diff:
```python
import functools
import math

import jax
import jax.numpy as jnp
from jax import lax
from jax.experimental import pallas as pl
from jax.experimental.pallas import tpu as pltpu
from jax.sharding import PartitionSpec as P

MESH = pl.DeviceIdType.MESH
LANES = 128
ROWS = 16
NT = (((1,), (1,)), ((), ()))


def kernel(
    dims,
    lengths,
    routing,
    cache_hbm,
    queries_hbm,
    fresh_hbm,
    residual_hbm,
    gain_hbm,
    router_hbm,
    gate_hbm,
    up_hbm,
    updated_out,
    hidden_out,
    cache_out,
    cache,
    queries,
    fresh,
    residual,
    gain,
    router,
    gate_w,
    up_w,
    residual_rows,
    stream,
    stream_rows,
    tiles,
    normed,
    columns,
    tokens,
    routes,
    gate_all,
    up_all,
    partial,
    arrived,
    load_sem,
    local_sem,
    stream_send,
    stream_recv,
    cache_send,
    cache_recv,
    route_send,
    route_recv,
    column_send,
    column_recv,
    sum_send,
    sum_recv,
):
    groups, tensors, span = dims
    mine = lax.axis_index("group")
    rank = lax.axis_index("tensor")
    pairs, slots, width = cache.shape
    head = width // 2
    seqs, cols = updated_out.shape
    per_seq = tensors // seqs
    seq = rank // per_seq
    part = lax.rem(rank, per_seq)
    heads = cols // per_seq // head
    share = heads // pairs
    blocks = cols // LANES
    own_blocks = blocks // groups
    experts = gate_w.shape[0]
    hidden = gate_w.shape[2]

    def tensor_peer(i):
        return lax.rem(rank + i, tensors)

    def group_peer(i):
        return lax.rem(mine + i, groups)

    def cache_copy(to, slot):
        return pltpu.make_async_remote_copy(
            src_ref=cache.at[:, pl.ds(pl.multiple_of(to * span, span), span), :],
            dst_ref=cache_out.at[pl.ds(slot * pairs, pairs)],
            send_sem=cache_send.at[to],
            recv_sem=cache_recv.at[slot],
            device_id={"tensor": to},
            device_id_type=MESH,
        )

    def stream_copy(to, slot):
        return pltpu.make_async_remote_copy(
            src_ref=stream.at[slot],
            dst_ref=stream.at[slot],
            send_sem=stream_send.at[to],
            recv_sem=stream_recv.at[slot],
            device_id={"tensor": to},
            device_id_type=MESH,
        )

    def route_copy(to, slot):
        return pltpu.make_async_remote_copy(
            src_ref=routes.at[slot],
            dst_ref=routes.at[slot],
            send_sem=route_send.at[to],
            recv_sem=route_recv.at[slot],
            device_id={"group": to},
            device_id_type=MESH,
        )

    def column_copy(to, slot):
        return pltpu.make_async_remote_copy(
            src_ref=normed.at[pl.ds(to * own_blocks, own_blocks)],
            dst_ref=columns.at[slot],
            send_sem=column_send.at[to],
            recv_sem=column_recv.at[slot],
            device_id={"group": to},
            device_id_type=MESH,
        )

    def sum_copy(to, slot):
        return pltpu.make_async_remote_copy(
            src_ref=partial.at[to],
            dst_ref=arrived.at[slot],
            send_sem=sum_send.at[to],
            recv_sem=sum_recv.at[slot],
            device_id={"group": to},
            device_id_type=MESH,
        )

    def each(count, step):
        def go(i, carry):
            step(i)
            return carry

        lax.fori_loop(1, count, go, 0)

    barrier = pltpu.get_barrier_semaphore()
    each(
        tensors,
        lambda i: pl.semaphore_signal(
            barrier, inc=1, device_id={"tensor": tensor_peer(i)}, device_id_type=MESH
        ),
    )
    each(
        groups,
        lambda i: pl.semaphore_signal(
            barrier, inc=1, device_id={"group": group_peer(i)}, device_id_type=MESH
        ),
    )

    loads = [
        pltpu.make_async_copy(source, target, load_sem.at[k])
        for k, (source, target) in enumerate(
            (
                (cache_hbm, cache),
                (queries_hbm.at[seq], queries),
                (fresh_hbm.at[seq], fresh),
                (residual_hbm, residual),
                (gain_hbm, gain),
                (router_hbm, router),
                (gate_hbm, gate_w),
                (up_hbm, up_w),
            )
        )
    ]
    for load in loads:
        load.start()
    for load in loads[:4]:
        load.wait()

    length = lengths[seq]
    fresh_rows = fresh[...].astype(jnp.float32)
    row_id = lax.broadcasted_iota(jnp.int32, fresh_rows.shape, 0)
    chunk = 128
    for p in range(pairs):
        own_row = jnp.sum(
            jnp.where(row_id == part * pairs + p, fresh_rows, 0.0), axis=0, keepdims=True
        )

        def place(c, carry, p=p, own_row=own_row):
            at = pl.ds(pl.multiple_of(c * chunk, chunk), chunk)
            slot_id = lax.broadcasted_iota(jnp.int32, (chunk, width), 0) + c * chunk
            cache[p, at, :] = jnp.where(
                slot_id == length, own_row, cache[p, at, :].astype(jnp.float32)
            ).astype(jnp.bfloat16)
            return carry

        lax.fori_loop(0, slots // chunk, place, 0)

    pick = (
        lax.broadcasted_iota(jnp.int32, (ROWS, queries.shape[0]), 1)
        == lax.broadcasted_iota(jnp.int32, (ROWS, queries.shape[0]), 0) + part * heads
    )
    own_queries = jnp.dot(
        pick.astype(jnp.float32).astype(jnp.bfloat16),
        queries[...],
        preferred_element_type=jnp.float32,
    ).astype(jnp.bfloat16)
    visible = lax.broadcasted_iota(jnp.int32, (ROWS, slots), 1) <= length
    out_row = lax.broadcasted_iota(jnp.int32, (ROWS, head), 0)
    attention = None
    for p in range(pairs):
        scores = lax.dot_general(
            own_queries, cache[p, :, :head], NT, preferred_element_type=jnp.float32
        ) * (1.0 / math.sqrt(head))
        scores = jnp.where(visible, scores, -1e30)
        peak = jnp.max(scores, axis=1, keepdims=True)
        weights = jnp.where(visible, jnp.exp(scores - peak), 0.0)
        denominator = jnp.sum(weights, axis=1, keepdims=True)
        weighted = jnp.dot(
            weights.astype(jnp.bfloat16), cache[p, :, head:], preferred_element_type=jnp.float32
        )
        result = weighted / denominator
        attention = result if p == 0 else jnp.where(out_row < p * share, attention, result)

    residual_rows[...] = jnp.zeros_like(residual_rows)
    for c in range(heads):
        at = pl.ds(pl.multiple_of(part * heads * LANES + c * LANES, LANES), LANES)
        residual_rows[c * seqs : (c + 1) * seqs, :] = residual[:, at].astype(jnp.float32)
    own_residual = residual_rows[pl.ds(seq, ROWS, stride=seqs), :]
    stream[rank] = (own_residual + attention).astype(jnp.bfloat16)

    sublane = lax.broadcasted_iota(jnp.int32, (seqs, LANES), 0)
    for k in range(routing.shape[0]):
        value = jnp.zeros((seqs, LANES), jnp.int32)
        for s in range(seqs):
            value = jnp.where(sublane == s, routing[k, s], value)
        routes[mine, k] = value

    pl.semaphore_wait(barrier, tensors + groups - 2)
    each(tensors, lambda i: stream_copy(tensor_peer(i), rank).start())
    each(groups, lambda i: route_copy(group_peer(i), mine).start())
    keep = pltpu.make_async_copy(
        cache.at[:, pl.ds(pl.multiple_of(rank * span, span), span), :],
        cache_out.at[pl.ds(rank * pairs, pairs)],
        local_sem,
    )
    keep.start()
    each(tensors, lambda i: cache_copy(tensor_peer(i), rank).start())
    for load in loads[4:]:
        load.wait()
    each(tensors, lambda i: stream_copy(rank, tensor_peer(i)).wait_recv())

    for k in range(tensors):
        stream_rows[k * ROWS : (k + 1) * ROWS, :] = stream[k].astype(jnp.float32)
    total = jnp.zeros((seqs, LANES), jnp.float32)
    for c in range(blocks):
        start = c // heads * ROWS + c % heads
        tile = stream_rows[pl.ds(start, seqs, stride=per_seq * ROWS), :]
        tiles[c] = tile
        total = total + tile * tile
        updated_out[:, c * LANES : (c + 1) * LANES] = tile.astype(jnp.bfloat16)
    scale = lax.rsqrt(jnp.sum(total, axis=1, keepdims=True) / cols + 1e-05)
    for c in range(blocks):
        normed[c] = (tiles[c] * scale * gain[c : c + 1, :]).astype(jnp.bfloat16)
    each(groups, lambda i: column_copy(group_peer(i), mine).start())
    columns[mine] = normed[pl.ds(mine * own_blocks, own_blocks)]

    logits = jnp.zeros((seqs, experts), jnp.float32)
    for c in range(blocks):
        logits = logits + lax.dot_general(
            normed[c],
            router[:, c * LANES : (c + 1) * LANES],
            NT,
            preferred_element_type=jnp.float32,
        )
    expert_id = lax.broadcasted_iota(jnp.int32, (seqs, experts), 1)
    chosen = [
        jnp.sum(
            jnp.where(routes[mine, k][:, :1] == expert_id, logits, 0.0), axis=1, keepdims=True
        )
        for k in range(2)
    ]
    gate_weights = [
        1.0 / (1.0 + jnp.exp(chosen[1] - chosen[0])),
        1.0 / (1.0 + jnp.exp(chosen[0] - chosen[1])),
    ]

    each(groups, lambda i: route_copy(mine, group_peer(i)).wait_recv())
    each(groups, lambda i: column_copy(mine, group_peer(i)).wait_recv())
    for c in range(own_blocks):
        tokens[:, c * LANES : (c + 1) * LANES] = (
            columns[:, c].astype(jnp.float32).reshape(groups * seqs, LANES).astype(jnp.bfloat16)
        )

    def products(e, carry):
        gate_all[e] = jnp.dot(tokens[...], gate_w[e], preferred_element_type=jnp.float32)
        up_all[e] = jnp.dot(tokens[...], up_w[e], preferred_element_type=jnp.float32)
        return carry

    lax.fori_loop(0, experts, products, 0)

    def choose(to):
        at = pl.ds(pl.multiple_of(to * seqs, seqs), seqs)
        for k in range(2):
            route = routes[to, k]
            route = jnp.concatenate([route] * (hidden // LANES), axis=1)
            for q, source in enumerate((gate_all, up_all)):
                value = source[0, at, :]
                for e in range(1, experts):
                    value = jnp.where(route == e, source[e, at, :], value)
                partial[to, 2 * k + q] = value.astype(jnp.bfloat16)

    def choose_and_send(i):
        choose(group_peer(i))

        @pl.when(i > 1)
        def _():
            sum_copy(group_peer(i - 1), mine).start()

    each(groups, choose_and_send)
    choose(mine)
    sum_copy(group_peer(groups - 1), mine).start()
    arrived[mine] = partial[mine]
    each(groups, lambda i: sum_copy(mine, group_peer(i)).wait_recv())

    for k in range(2):
        sums = []
        for q in range(2):
            value = arrived[0, 2 * k + q].astype(jnp.float32)
            for s in range(1, groups):
                value = value + arrived[s, 2 * k + q].astype(jnp.float32)
            sums.append(value)
        silu = sums[0] / (1.0 + jnp.exp(-sums[0]))
        hidden_out[k] = (gate_weights[k] * silu * sums[1]).astype(jnp.bfloat16)

    each(groups, lambda i: route_copy(group_peer(i), mine).wait_send())
    each(groups, lambda i: column_copy(group_peer(i), mine).wait_send())
    each(groups, lambda i: sum_copy(group_peer(i), mine).wait_send())
    each(tensors, lambda i: stream_copy(tensor_peer(i), rank).wait_send())
    each(tensors, lambda i: cache_copy(tensor_peer(i), rank).wait_send())
    each(tensors, lambda i: cache_copy(rank, tensor_peer(i)).wait_recv())
    keep.wait()


def body(
    groups,
    tensors,
    key_value_cache,
    queries,
    fresh_key_value,
    lengths,
    residual,
    norm_gain,
    router_weight,
    routing,
    expert_gate,
    expert_up,
):
    pairs, slots, width = key_value_cache.shape
    seqs, q_heads, head = queries.shape
    kv_heads = fresh_key_value.shape[1]
    cols = residual.shape[1]
    experts, own_cols, hidden = expert_gate.shape
    span = slots // tensors
    bf16, f32, i32 = jnp.bfloat16, jnp.float32, jnp.int32
    dma = pltpu.SemaphoreType.DMA
    hbm = pl.BlockSpec(memory_space=pltpu.HBM)
    vmem = pl.BlockSpec(memory_space=pltpu.VMEM)
    smem = pl.BlockSpec(memory_space=pltpu.SMEM)
    updated, hidden_units, new_cache = pl.pallas_call(
        functools.partial(kernel, (groups, tensors, span)),
        out_shape=(
            jax.ShapeDtypeStruct((seqs, cols), bf16),
            jax.ShapeDtypeStruct((2, seqs, hidden), bf16),
            jax.ShapeDtypeStruct((seqs * kv_heads, span, width), bf16),
        ),
        in_specs=[smem] * 2 + [hbm] * 8,
        out_specs=(vmem, vmem, hbm),
        scratch_shapes=[
            pltpu.VMEM((pairs, slots, width), bf16),
            pltpu.VMEM((q_heads, head), bf16),
            pltpu.VMEM((kv_heads, width), bf16),
            pltpu.VMEM((seqs, cols), bf16),
            pltpu.VMEM((cols // LANES, LANES), f32),
            pltpu.VMEM((experts, cols), bf16),
            pltpu.VMEM(expert_gate.shape, bf16),
            pltpu.VMEM(expert_up.shape, bf16),
            pltpu.VMEM((ROWS * seqs, LANES), f32),
            pltpu.VMEM((tensors, ROWS, LANES), bf16),
            pltpu.VMEM((tensors * ROWS, LANES), f32),
            pltpu.VMEM((cols // LANES, seqs, LANES), f32),
            pltpu.VMEM((cols // LANES, seqs, LANES), bf16),
            pltpu.VMEM((groups, own_cols // LANES, seqs, LANES), bf16),
            pltpu.VMEM((groups * seqs, own_cols), bf16),
            pltpu.VMEM((groups, 2, seqs, LANES), i32),
            pltpu.VMEM((experts, groups * seqs, hidden), f32),
            pltpu.VMEM((experts, groups * seqs, hidden), f32),
            pltpu.VMEM((groups, 4, seqs, hidden), bf16),
            pltpu.VMEM((groups, 4, seqs, hidden), bf16),
            dma((8,)),
            dma(()),
            dma((tensors,)),
            dma((tensors,)),
            dma((tensors,)),
            dma((tensors,)),
            dma((groups,)),
            dma((groups,)),
            dma((groups,)),
            dma((groups,)),
            dma((groups,)),
            dma((groups,)),
        ],
        compiler_params=pltpu.CompilerParams(collective_id=0, has_side_effects=True),
    )(
        lengths,
        routing.T,
        key_value_cache,
        queries,
        fresh_key_value,
        residual,
        norm_gain.reshape(cols // LANES, LANES),
        router_weight.T,
        expert_gate,
        expert_up,
    )
    return (
        updated,
        jnp.swapaxes(hidden_units, 0, 1),
        new_cache.reshape(seqs, kv_heads, span, width),
    )


def solution(mesh):
    in_specs = (
        P(("group", "tensor"), None, None),
        P("group", None, None),
        P("group", None, None),
        P("group"),
        P("group", None),
        P(),
        P(),
        P("group", None),
        P(None, "group", "tensor"),
        P(None, "group", "tensor"),
    )
    out_specs = (P("group", None), P("group", None, "tensor"), P("group", None, "tensor", None))
    return jax.shard_map(
        functools.partial(body, mesh.shape["group"], mesh.shape["tensor"]),
        mesh=mesh,
        in_specs=in_specs,
        out_specs=out_specs,
        check_vma=False,
    )
```

time: 115 us -> 55.1 us (0.48)
  the two profiles are of different devices: /device:TPU:1 before, /device:TPU:15 now
where the time goes in v1:
time: 55.1 us; the launch traced here: 54.9 us
  Pallas kernels  49.1 us (89%)
  local copies, waits for them, and re-layouts  5.1 us (9%)
  between operations  0.64 us (1%)
    pallas_call x1, Pallas kernels, body(): pl.pallas_call(functools.partial(kernel, (groups, tensors, span)), out_sh...  49.1 us
    unnamed x3, local copies, waits for them, and re-layouts  5.1 us

profile of v1, /device:TPU:15, one launch (start us, length us, event | category | flops | bytes accessed | tf_op | source)
XLA Modules:
  0.0 54.9 jit_solution(5889829729638336240)
XLA Ops:
  0.6 49.1 %shard_map.121 = (bf16[8,6144]{1,0:T(8,128)(2,1)}, bf16[2,8,256]{2,1,0:T(8,128)(2,1)}, bf16[64,32,256]{2,1,0:T(8,128)(2,1)}) custom-call(s32[8]{0:T(128)} %lengths.1, s32[2,8]{1,0:T(2,128)} %bitcast.9, bf16[2,1024,256]{2,1,0:T(8,128)(2,1)} %cache_hbm.1, bf16[8,48,128]{2,1,0:T(8,128)(2,1)} %queries_hbm.1, bf16[8,8,256]{2,1,0:T(8,128)(2,1)} %fresh_hbm.1, ...), custom_call_target="tpu_custom_call" | custom-call | tf_op jit(solution)/shard_map/pallas_call | solution.py:368
  49.8 1.3 %copy.13 = bf16[8,2,256]{2,1,0:T(2,128)(2,1)} copy(bf16[8,2,256]{2,0,1:T(8,128)(2,1)} %bitcast.8) | data formatting | bytes 16384
  51.1 1.5 %copy.16 = bf16[8,6144]{1,0:T(8,128)(2,1)} copy(bf16[8,6144]{1,0:T(8,128)(2,1)} %get-tuple-element.15) | data formatting | bytes 196608
  52.6 2.3 %copy.17 = bf16[8,8,32,256]{3,2,1,0:T(8,128)(2,1)} copy(bf16[8,8,32,256]{3,2,1,0:T(8,128)(2,1)} %bitcast.5) | data formatting | bytes 2097152

commit v2 on v1

v2 whole, which is shorter than its diff:
```python
import functools
import math

import jax
import jax.numpy as jnp
from jax import lax
from jax.experimental import pallas as pl
from jax.experimental.pallas import tpu as pltpu
from jax.sharding import PartitionSpec as P

MESH = pl.DeviceIdType.MESH
LANES = 128
ROWS = 16
NT = (((1,), (1,)), ((), ()))


def kernel(
    dims,
    lengths_hbm,
    routing_hbm,
    cache_hbm,
    queries_hbm,
    fresh_hbm,
    residual_hbm,
    gain_hbm,
    router_hbm,
    gate_hbm,
    up_hbm,
    updated_out,
    hidden_out,
    cache_out,
    lengths,
    routing,
    cache,
    queries,
    fresh,
    residual,
    gain,
    router,
    gate_w,
    up_w,
    residual_rows,
    stream,
    stream_rows,
    raw,
    scaled,
    normed,
    columns,
    tokens,
    routes,
    gate_all,
    up_all,
    partial,
    arrived,
    load_sem,
    local_sem,
    stream_send,
    stream_recv,
    raw_send,
    raw_recv,
    cache_send,
    cache_recv,
    route_send,
    route_recv,
    column_send,
    column_recv,
    sum_send,
    sum_recv,
):
    groups, tensors, span = dims
    mine = lax.axis_index("group")
    rank = lax.axis_index("tensor")
    pairs, slots, width = cache.shape
    head = width // 2
    seqs, cols = updated_out.shape
    parts = tensors // seqs
    seq = rank // parts
    part = lax.rem(rank, parts)
    heads = cols // parts // head
    share = heads // pairs
    blocks = cols // LANES
    own_blocks = blocks // groups
    pieces = groups // parts
    experts = gate_w.shape[0]
    hidden = gate_w.shape[2]
    home = mine // pieces
    at_home = home == part

    def tensor_peer(i):
        return lax.rem(rank + i, tensors)

    def group_peer(i):
        return lax.rem(mine + i, groups)

    def seq_peer(i):
        return lax.rem(seq + i, seqs)

    def part_peer(i):
        return lax.rem(part + i, parts)

    def remote(source, target, send, recv, **to):
        return pltpu.make_async_remote_copy(
            src_ref=source,
            dst_ref=target,
            send_sem=send,
            recv_sem=recv,
            device_id=to,
            device_id_type=MESH,
        )

    def cache_copy(to):
        return remote(
            cache.at[:, pl.ds(pl.multiple_of(to * span, span), span), :],
            cache_out.at[pl.ds(rank * pairs, pairs)],
            cache_send,
            cache_recv,
            tensor=to,
        )

    def stream_copy(to):
        return remote(
            stream.at[seq], stream.at[seq], stream_send, stream_recv, tensor=to * parts + part
        )

    def raw_copy(to):
        return remote(raw.at[part], raw.at[part], raw_send, raw_recv, tensor=seq * parts + to)

    def route_copy(to):
        return remote(routes.at[mine], routes.at[mine], route_send, route_recv, group=to)

    def column_copy(piece, to):
        return remote(
            scaled.at[pl.ds(piece * own_blocks, own_blocks)],
            columns.at[mine],
            column_send,
            column_recv,
            group=part * pieces + piece,
            tensor=seq * parts + to,
        )

    def sum_copy(to):
        return remote(partial.at[to], arrived.at[mine], sum_send, sum_recv, group=to)

    def signal(**to):
        pl.semaphore_signal(barrier, inc=1, device_id=to, device_id_type=MESH)

    def each(count, step):
        def go(i, carry):
            step(i)
            return carry

        lax.fori_loop(1, count, go, 0)

    loads = [
        pltpu.make_async_copy(source, target, load_sem.at[k])
        for k, (source, target) in enumerate(
            (
                (cache_hbm, cache),
                (lengths_hbm, lengths),
                (queries_hbm.at[seq], queries),
                (fresh_hbm.at[seq], fresh),
                (residual_hbm, residual),
                (routing_hbm, routing),
                (gain_hbm, gain),
                (router_hbm, router),
                (gate_hbm, gate_w),
                (up_hbm, up_w),
            )
        )
    ]
    for load in loads:
        load.start()

    barrier = pltpu.get_barrier_semaphore()
    for i in range(1, tensors):
        signal(tensor=tensor_peer(i))
    for i in range(1, groups):
        signal(group=group_peer(i))

    @pl.when(jnp.logical_not(at_home))
    def _():
        for i in range(groups):
            signal(group=i, tensor=seq * parts + home)

    @pl.when(at_home)
    def _():
        each(groups, lambda i: signal(group=group_peer(i)))

    for load in loads[:6]:
        load.wait()

    length = lengths[seq]
    fresh_rows = fresh[...].astype(jnp.float32)
    row_id = lax.broadcasted_iota(jnp.int32, fresh_rows.shape, 0)
    chunk = 128
    for p in range(pairs):
        own_row = jnp.sum(
            jnp.where(row_id == part * pairs + p, fresh_rows, 0.0), axis=0, keepdims=True
        )

        def place(c, carry, p=p, own_row=own_row):
            at = pl.ds(pl.multiple_of(c * chunk, chunk), chunk)
            slot_id = lax.broadcasted_iota(jnp.int32, (chunk, width), 0) + c * chunk
            cache[p, at, :] = jnp.where(
                slot_id == length, own_row, cache[p, at, :].astype(jnp.float32)
            ).astype(jnp.bfloat16)
            return carry

        lax.fori_loop(0, slots // chunk, place, 0)

    pick = (
        lax.broadcasted_iota(jnp.int32, (ROWS, queries.shape[0]), 1)
        == lax.broadcasted_iota(jnp.int32, (ROWS, queries.shape[0]), 0) + part * heads
    )
    own_queries = jnp.dot(
        pick.astype(jnp.float32).astype(jnp.bfloat16),
        queries[...],
        preferred_element_type=jnp.float32,
    ).astype(jnp.bfloat16)
    visible = lax.broadcasted_iota(jnp.int32, (ROWS, slots), 1) <= length
    out_row = lax.broadcasted_iota(jnp.int32, (ROWS, head), 0)
    attention = None
    for p in range(pairs):
        scores = lax.dot_general(
            own_queries, cache[p, :, :head], NT, preferred_element_type=jnp.float32
        ) * (1.0 / math.sqrt(head))
        scores = jnp.where(visible, scores, -1e30)
        peak = jnp.max(scores, axis=1, keepdims=True)
        weights = jnp.where(visible, jnp.exp(scores - peak), 0.0)
        denominator = jnp.sum(weights, axis=1, keepdims=True)
        weighted = jnp.dot(
            weights.astype(jnp.bfloat16), cache[p, :, head:], preferred_element_type=jnp.float32
        )
        result = weighted / denominator
        attention = result if p == 0 else jnp.where(out_row < p * share, attention, result)

    residual_rows[...] = jnp.zeros_like(residual_rows)
    for c in range(heads):
        at = pl.ds(pl.multiple_of(part * heads * LANES + c * LANES, LANES), LANES)
        residual_rows[c * seqs : (c + 1) * seqs, :] = residual[:, at].astype(jnp.float32)
    own_residual = residual_rows[pl.ds(seq, ROWS, stride=seqs), :]
    stream[seq] = (own_residual + attention).astype(jnp.bfloat16)

    sublane = lax.broadcasted_iota(jnp.int32, (seqs, LANES), 0)
    for k in range(routing.shape[0]):
        value = jnp.zeros((seqs, LANES), jnp.int32)
        for s in range(seqs):
            value = jnp.where(sublane == s, routing[k, s], value)
        routes[mine, k] = value

    pl.semaphore_wait(barrier, tensors + groups - 2 + groups - jnp.where(at_home, 1, 0))
    each(seqs, lambda i: stream_copy(seq_peer(i)).start())
    each(groups, lambda i: route_copy(group_peer(i)).start())
    keep = pltpu.make_async_copy(
        cache.at[:, pl.ds(pl.multiple_of(rank * span, span), span), :],
        cache_out.at[pl.ds(rank * pairs, pairs)],
        local_sem,
    )
    keep.start()
    each(tensors, lambda i: cache_copy(tensor_peer(i)).start())
    for load in loads[6:]:
        load.wait()
    others = stream.at[pl.ds(0, seqs - 1)]
    remote(others, others, stream_send, stream_recv, tensor=rank).wait_recv()

    for k in range(seqs):
        stream_rows[k * ROWS : (k + 1) * ROWS, :] = stream[k].astype(jnp.float32)
    for c in range(heads):
        tile = stream_rows[pl.ds(c, seqs, stride=ROWS), :]
        raw[part, c] = tile.astype(jnp.bfloat16)
        scaled[c] = (tile * gain[pl.ds(part * heads + c, 1), :]).astype(jnp.bfloat16)
    for piece in range(pieces):
        for i in range(1, parts):
            column_copy(piece, part_peer(i)).start()

        @pl.when(part * pieces + piece != mine)
        def _():
            column_copy(piece, part).start()

    own_columns = pltpu.make_async_copy(
        scaled.at[pl.ds(lax.rem(mine, pieces) * own_blocks, own_blocks)],
        columns.at[mine],
        column_recv,
    )

    @pl.when(at_home)
    def _():
        own_columns.start()

    each(parts, lambda i: raw_copy(part_peer(i)).start())

    other_routes = routes.at[pl.ds(0, groups - 1)]
    remote(other_routes, other_routes, route_send, route_recv, group=mine).wait_recv()
    remote(columns, columns, column_send, column_recv, group=mine).wait_recv()
    for c in range(own_blocks):
        tokens[:, c * LANES : (c + 1) * LANES] = (
            columns[:, c].astype(jnp.float32).reshape(groups * seqs, LANES).astype(jnp.bfloat16)
        )
    for e in range(experts):
        gate_all[e] = jnp.dot(tokens[...], gate_w[e], preferred_element_type=jnp.float32)
        up_all[e] = jnp.dot(tokens[...], up_w[e], preferred_element_type=jnp.float32)

    def choose(to):
        at = pl.ds(pl.multiple_of(to * seqs, seqs), seqs)
        for k in range(2):
            route = routes[to, k]
            route = jnp.concatenate([route] * (hidden // LANES), axis=1)
            for q, source in enumerate((gate_all, up_all)):
                value = source[0, at, :]
                for e in range(1, experts):
                    value = jnp.where(route == e, source[e, at, :], value)
                partial[to, 2 * k + q] = value.astype(jnp.bfloat16)

    def choose_and_send(i):
        choose(group_peer(i))

        @pl.when(i > 1)
        def _():
            sum_copy(group_peer(i - 1)).start()

    each(groups, choose_and_send)
    choose(mine)
    sum_copy(group_peer(groups - 1)).start()
    arrived[mine] = partial[mine]

    other_parts = raw.at[pl.ds(0, parts - 1)]
    remote(other_parts, other_parts, raw_send, raw_recv, group=mine).wait_recv()
    total = jnp.zeros((seqs, LANES), jnp.float32)
    for c in range(blocks):
        value = raw[c // heads, c % heads]
        updated_out[:, c * LANES : (c + 1) * LANES] = value
        value = value.astype(jnp.float32)
        total = total + value * value
    scale = lax.rsqrt(jnp.sum(total, axis=1, keepdims=True) / cols + 1e-05)
    for c in range(blocks):
        value = raw[c // heads, c % heads].astype(jnp.float32)
        normed[:, c * LANES : (c + 1) * LANES] = (value * scale * gain[c : c + 1, :]).astype(
            jnp.bfloat16
        )
    logits = lax.dot_general(normed[...], router[...], NT, preferred_element_type=jnp.float32)
    expert_id = lax.broadcasted_iota(jnp.int32, (seqs, experts), 1)
    chosen = [
        jnp.sum(
            jnp.where(routes[mine, k][:, :1] == expert_id, logits, 0.0), axis=1, keepdims=True
        )
        for k in range(2)
    ]
    gate_weights = [
        1.0 / (1.0 + jnp.exp(chosen[1] - chosen[0])),
        1.0 / (1.0 + jnp.exp(chosen[0] - chosen[1])),
    ]

    other_sums = arrived.at[pl.ds(0, groups - 1)]
    remote(other_sums, other_sums, sum_send, sum_recv, group=mine).wait_recv()
    units = []
    for k in range(2):
        sums = []
        for q in range(2):
            value = arrived[0, 2 * k + q].astype(jnp.float32)
            for s in range(1, groups):
                value = value + arrived[s, 2 * k + q].astype(jnp.float32)
            sums.append(value * scale)
        silu = sums[0] / (1.0 + jnp.exp(-sums[0]))
        units.append(gate_weights[k] * silu * sums[1])
    for s in range(seqs):
        hidden_out[s] = jnp.concatenate([unit[s : s + 1] for unit in units], axis=0).astype(
            jnp.bfloat16
        )

    remote(others, others, stream_send, stream_recv, tensor=rank).wait_send()
    remote(other_routes, other_routes, route_send, route_recv, group=mine).wait_send()
    remote(other_parts, other_parts, raw_send, raw_recv, group=mine).wait_send()
    remote(other_sums, other_sums, sum_send, sum_recv, group=mine).wait_send()
    most = columns.at[pl.ds(0, groups - 1)]
    remote(most, most, column_send, column_recv, group=mine).wait_send()

    @pl.when(jnp.logical_not(at_home))
    def _():
        one = columns.at[0]
        remote(one, one, column_send, column_recv, group=mine).wait_send()

    most_cache = cache_out.at[pl.ds(0, (tensors - 1) * pairs)]
    remote(most_cache, most_cache, cache_send, cache_recv, tensor=rank).wait_send()
    keep.wait()
    remote(most_cache, most_cache, cache_send, cache_recv, tensor=rank).wait_recv()


def write_out(updated, hidden_units, cache, updated_hbm, hidden_hbm, cache_hbm, sems):
    copies = [
        pltpu.make_async_copy(source, target, sems.at[k])
        for k, (source, target) in enumerate(
            ((cache, cache_hbm), (updated, updated_hbm), (hidden_units, hidden_hbm))
        )
    ]
    for copy in copies:
        copy.start()
    for copy in copies:
        copy.wait()


def body(
    groups,
    tensors,
    key_value_cache,
    queries,
    fresh_key_value,
    lengths,
    residual,
    norm_gain,
    router_weight,
    routing,
    expert_gate,
    expert_up,
):
    pairs, slots, width = key_value_cache.shape
    seqs, q_heads, head = queries.shape
    kv_heads = fresh_key_value.shape[1]
    cols = residual.shape[1]
    experts, own_cols, hidden = expert_gate.shape
    span = slots // tensors
    parts = tensors // seqs
    heads = cols // parts // head
    bf16, f32, i32 = jnp.bfloat16, jnp.float32, jnp.int32
    dma = pltpu.SemaphoreType.DMA
    hbm = pl.BlockSpec(memory_space=pltpu.HBM)
    vmem = pl.BlockSpec(memory_space=pltpu.VMEM)
    updated, hidden_units, new_cache = pl.pallas_call(
        functools.partial(kernel, (groups, tensors, span)),
        out_shape=(
            pltpu.VMEM((seqs, cols), bf16),
            pltpu.VMEM((seqs, 2, hidden), bf16),
            pltpu.VMEM((seqs * kv_heads, span, width), bf16),
        ),
        in_specs=[hbm] * 10,
        out_specs=(vmem, vmem, vmem),
        scratch_shapes=[
            pltpu.SMEM((seqs,), i32),
            pltpu.SMEM((2, seqs), i32),
            pltpu.VMEM((pairs, slots, width), bf16),
            pltpu.VMEM((q_heads, head), bf16),
            pltpu.VMEM((kv_heads, width), bf16),
            pltpu.VMEM((seqs, cols), bf16),
            pltpu.VMEM((cols // LANES, LANES), f32),
            pltpu.VMEM((experts, cols), bf16),
            pltpu.VMEM(expert_gate.shape, bf16),
            pltpu.VMEM(expert_up.shape, bf16),
            pltpu.VMEM((ROWS * seqs, LANES), f32),
            pltpu.VMEM((seqs, ROWS, LANES), bf16),
            pltpu.VMEM((seqs * ROWS, LANES), f32),
            pltpu.VMEM((parts, heads, seqs, LANES), bf16),
            pltpu.VMEM((heads, seqs, LANES), bf16),
            pltpu.VMEM((seqs, cols), bf16),
            pltpu.VMEM((groups, own_cols // LANES, seqs, LANES), bf16),
            pltpu.VMEM((groups * seqs, own_cols), bf16),
            pltpu.VMEM((groups, 2, seqs, LANES), i32),
            pltpu.VMEM((experts, groups * seqs, hidden), f32),
            pltpu.VMEM((experts, groups * seqs, hidden), f32),
            pltpu.VMEM((groups, 4, seqs, hidden), bf16),
            pltpu.VMEM((groups, 4, seqs, hidden), bf16),
            dma((10,)),
        ]
        + [dma(())] * 13,
        compiler_params=pltpu.CompilerParams(
            collective_id=0, has_side_effects=True
        ),
    )(
        lengths,
        routing.T,
        key_value_cache,
        queries,
        fresh_key_value,
        residual,
        norm_gain.reshape(cols // LANES, LANES),
        router_weight.T,
        expert_gate,
        expert_up,
    )
    updated, hidden_units, new_cache = pl.pallas_call(
        write_out,
        out_shape=(
            jax.ShapeDtypeStruct(updated.shape, bf16),
            jax.ShapeDtypeStruct(hidden_units.shape, bf16),
            jax.ShapeDtypeStruct(new_cache.shape, bf16),
        ),
        in_specs=[vmem] * 3,
        out_specs=(hbm,) * 3,
        scratch_shapes=[dma((3,))],
        compiler_params=pltpu.CompilerParams(vmem_limit_bytes=4 << 20),
    )(updated, hidden_units, new_cache)
    return (
        updated,
        hidden_units,
        new_cache.reshape(seqs, kv_heads, span, width),
    )


def solution(mesh):
    in_specs = (
        P(("group", "tensor"), None, None),
        P("group", None, None),
        P("group", None, None),
        P("group"),
        P("group", None),
        P(),
        P(),
        P("group", None),
        P(None, "group", "tensor"),
        P(None, "group", "tensor"),
    )
    out_specs = (P("group", None), P("group", None, "tensor"), P("group", None, "tensor", None))
    return jax.shard_map(
        functools.partial(body, mesh.shape["group"], mesh.shape["tensor"]),
        mesh=mesh,
        in_specs=in_specs,
        out_specs=out_specs,
        check_vma=False,
    )
```

time: 55.1 us -> 43.1 us (0.78)
  the two profiles are of different devices: /device:TPU:15 before, /device:TPU:17 now
where the time goes in v2:
time: 43.1 us; the launch traced here: 43 us
  Pallas kernels  42.4 us (98%)
  between operations  0.64 us (1%)
    pallas_call x1, Pallas kernels, body(): pl.pallas_call(functools.partial(kernel, (groups, tensors, span)), out_sh...  41.4 us
    pallas_call x1, Pallas kernels, body(): pl.pallas_call(write_out, out_shape=(jax.ShapeDtypeStruct(updated.shape,...  1.02 us

profile of v2, /device:TPU:17, one launch (start us, length us, event | category | flops | bytes accessed | tf_op | source)
XLA Modules:
  0.0 43.0 jit_solution(13241246715860078098)
XLA Ops:
  0.6 41.4 %shard_map.121 = (bf16[8,6144]{1,0:T(8,128)(2,1)S(1)}, bf16[8,2,256]{2,1,0:T(2,128)(2,1)S(1)}, bf16[64,32,256]{2,1,0:T(8,128)(2,1)S(1)}) custom-call(s32[8]{0:T(128)} %lengths_hbm.1, s32[2,8]{1,0:T(2,128)} %bitcast.6, bf16[2,1024,256]{2,1,0:T(8,128)(2,1)} %cache_hbm.1, bf16[8,48,128]{2,1,0:T(8,128)(2,1)} %queries_hbm.1, bf16[8,8,256]{2,1,0:T(8,128)(2,1)} %fresh_hbm.1, ...), custom_call_target="tpu_custom_call" | custom-call | tf_op jit(solution)/shard_map/pallas_call | solution.py:427
  42.0 1.0 %shard_map.122 = (bf16[8,6144]{1,0:T(8,128)(2,1)}, bf16[8,2,256]{2,1,0:T(2,128)(2,1)}, bf16[64,32,256]{2,1,0:T(8,128)(2,1)}) custom-call(bf16[8,6144]{1,0:T(8,128)(2,1)S(1)} %get-tuple-element.9.updated, bf16[8,2,256]{2,1,0:T(2,128)(2,1)S(1)} %get-tuple-element.10.hidden_units, bf16[64,32,256]{2,1,0:T(8,128)(2,1)S(1)} %get-tuple-element.11.cache), custom_call_target="tpu_custom_call" | custom-call | tf_op jit(solution)/shard_map/pallas_call | solution.py:478

commit v3 on v2

--- a/solution.py
+++ b/solution.py
@@ -12,6 +12,10 @@
 LANES = 128
 ROWS = 16
 NT = (((1,), (1,)), ((), ()))
+
+
+def FIRST(down, along):
+    return along == 0
 
 
 def kernel(
@@ -50,6 +54,9 @@
     routes,
     gate_all,
     up_all,
+    pair_out,
+    pair_in,
+    pair_own,
     partial,
     arrived,
     load_sem,
@@ -64,6 +71,8 @@
     route_recv,
     column_send,
     column_recv,
+    pair_send,
+    pair_recv,
     sum_send,
     sum_recv,
 ):
@@ -83,11 +92,10 @@
     pieces = groups // parts
     experts = gate_w.shape[0]
     hidden = gate_w.shape[2]
-    home = mine // pieces
-    at_home = home == part
-
-    def tensor_peer(i):
-        return lax.rem(rank + i, tensors)
+    chips = groups // 2
+    chip = mine // 2
+    core = lax.rem(mine, 2)
+    lower = mine < chips
 
     def group_peer(i):
         return lax.rem(mine + i, groups)
@@ -97,6 +105,17 @@
 
     def part_peer(i):
         return lax.rem(part + i, parts)
+
+    def chip_peer(i):
+        return lax.rem(chip + i, chips)
+
+    def tensor_peer(down, along):
+        return lax.rem(seq + down, seqs) * parts + lax.rem(part + along, parts)
+
+    offsets = sorted(
+        ((down, along) for down in range(seqs) for along in range(parts) if down or along),
+        key=lambda o: -min(o[0], seqs - o[0]) - min(o[1], parts - o[1]),
+    )
 
     def remote(source, target, send, recv, **to):
         return pltpu.make_async_remote_copy(
@@ -128,18 +147,19 @@
     def route_copy(to):
         return remote(routes.at[mine], routes.at[mine], route_send, route_recv, group=to)
 
-    def column_copy(piece, to):
+    def column_copy(to):
         return remote(
-            scaled.at[pl.ds(piece * own_blocks, own_blocks)],
+            scaled.at[pl.ds(to * own_blocks, own_blocks)],
             columns.at[mine],
             column_send,
             column_recv,
-            group=part * pieces + piece,
-            tensor=seq * parts + to,
+            group=to,
         )
 
     def sum_copy(to):
-        return remote(partial.at[to], arrived.at[mine], sum_send, sum_recv, group=to)
+        return remote(
+            partial.at[to], arrived.at[chip], sum_send, sum_recv, group=2 * to + core
+        )
 
     def signal(**to):
         pl.semaphore_signal(barrier, inc=1, device_id=to, device_id_type=MESH)
@@ -172,19 +192,8 @@
         load.start()
 
     barrier = pltpu.get_barrier_semaphore()
-    for i in range(1, tensors):
-        signal(tensor=tensor_peer(i))
-    for i in range(1, groups):
-        signal(group=group_peer(i))
-
-    @pl.when(jnp.logical_not(at_home))
-    def _():
-        for i in range(groups):
-            signal(group=i, tensor=seq * parts + home)
-
-    @pl.when(at_home)
-    def _():
-        each(groups, lambda i: signal(group=group_peer(i)))
+    for offset in offsets:
+        signal(tensor=tensor_peer(*offset))
 
     for load in loads[:6]:
         load.wait()
@@ -248,50 +257,81 @@
             value = jnp.where(sublane == s, routing[k, s], value)
         routes[mine, k] = value
 
-    pl.semaphore_wait(barrier, tensors + groups - 2 + groups - jnp.where(at_home, 1, 0))
+    pl.semaphore_wait(barrier, tensors - 1 + jnp.where(lower, 0, chips))
     each(seqs, lambda i: stream_copy(seq_peer(i)).start())
-    each(groups, lambda i: route_copy(group_peer(i)).start())
+
+    @pl.when(lower)
+    def _():
+        for i in range(chips, groups):
+            signal(group=i)
+
+    @pl.when(jnp.logical_not(lower))
+    def _():
+        for i in range(chips):
+            signal(group=i)
+
     keep = pltpu.make_async_copy(
         cache.at[:, pl.ds(pl.multiple_of(rank * span, span), span), :],
         cache_out.at[pl.ds(rank * pairs, pairs)],
         local_sem,
     )
     keep.start()
-    each(tensors, lambda i: cache_copy(tensor_peer(i)).start())
+    for offset in offsets:
+        if FIRST(*offset):
+            cache_copy(tensor_peer(*offset)).start()
     for load in loads[6:]:
         load.wait()
     others = stream.at[pl.ds(0, seqs - 1)]
     remote(others, others, stream_send, stream_recv, tensor=rank).wait_recv()
 
+    def scale_part(at):
+        for c in range(heads):
+            tile = raw[at, c].astype(jnp.float32)
+            scaled[at * heads + c] = (tile * gain[pl.ds(at * heads + c, 1), :]).astype(
+                jnp.bfloat16
+            )
+
     for k in range(seqs):
         stream_rows[k * ROWS : (k + 1) * ROWS, :] = stream[k].astype(jnp.float32)
     for c in range(heads):
-        tile = stream_rows[pl.ds(c, seqs, stride=ROWS), :]
-        raw[part, c] = tile.astype(jnp.bfloat16)
-        scaled[c] = (tile * gain[pl.ds(part * heads + c, 1), :]).astype(jnp.bfloat16)
-    for piece in range(pieces):
-        for i in range(1, parts):
-            column_copy(piece, part_peer(i)).start()
-
-        @pl.when(part * pieces + piece != mine)
-        def _():
-            column_copy(piece, part).start()
-
-    own_columns = pltpu.make_async_copy(
-        scaled.at[pl.ds(lax.rem(mine, pieces) * own_blocks, own_blocks)],
-        columns.at[mine],
-        column_recv,
-    )
-
-    @pl.when(at_home)
+        raw[part, c] = stream_rows[pl.ds(c, seqs, stride=ROWS), :].astype(jnp.bfloat16)
+    each(parts, lambda i: raw_copy(part_peer(i)).start())
+    for offset in offsets:
+        if not FIRST(*offset):
+            cache_copy(tensor_peer(*offset)).start()
+    scale_part(part)
+
+    @pl.when(lower)
     def _():
-        own_columns.start()
-
-    each(parts, lambda i: raw_copy(part_peer(i)).start())
+        pl.semaphore_wait(barrier, chips)
+        signal(group=groups - 1 - mine)
+
+    @pl.when(jnp.logical_not(lower))
+    def _():
+        pl.semaphore_wait(barrier, 1)
+
+    each(groups, lambda i: route_copy(group_peer(i)).start())
+    def send_part(at):
+        for piece in range(pieces):
+            to = at * pieces + piece
+
+            @pl.when(to != mine)
+            def _():
+                column_copy(to).start()
+
+    send_part(part)
+    other_parts = raw.at[pl.ds(0, parts - 1)]
+    remote(other_parts, other_parts, raw_send, raw_recv, group=mine).wait_recv()
+    for i in range(1, parts):
+        scale_part(part_peer(i))
+    for i in range(1, parts):
+        send_part(part_peer(i))
+    columns[mine] = scaled[pl.ds(mine * own_blocks, own_blocks)]
 
     other_routes = routes.at[pl.ds(0, groups - 1)]
     remote(other_routes, other_routes, route_send, route_recv, group=mine).wait_recv()
-    remote(columns, columns, column_send, column_recv, group=mine).wait_recv()
+    most = columns.at[pl.ds(0, groups - 1)]
+    remote(most, most, column_send, column_recv, group=mine).wait_recv()
     for c in range(own_blocks):
         tokens[:, c * LANES : (c + 1) * LANES] = (
             columns[:, c].astype(jnp.float32).reshape(groups * seqs, LANES).astype(jnp.bfloat16)
@@ -300,31 +340,46 @@
         gate_all[e] = jnp.dot(tokens[...], gate_w[e], preferred_element_type=jnp.float32)
         up_all[e] = jnp.dot(tokens[...], up_w[e], preferred_element_type=jnp.float32)
 
-    def choose(to):
-        at = pl.ds(pl.multiple_of(to * seqs, seqs), seqs)
+    def choose(to, target, at):
+        rows = pl.ds(pl.multiple_of(to * seqs, seqs), seqs)
         for k in range(2):
             route = routes[to, k]
             route = jnp.concatenate([route] * (hidden // LANES), axis=1)
             for q, source in enumerate((gate_all, up_all)):
-                value = source[0, at, :]
+                value = source[0, rows, :]
                 for e in range(1, experts):
-                    value = jnp.where(route == e, source[e, at, :], value)
-                partial[to, 2 * k + q] = value.astype(jnp.bfloat16)
-
-    def choose_and_send(i):
-        choose(group_peer(i))
+                    value = jnp.where(route == e, source[e, rows, :], value)
+                target[at, 2 * k + q] = value.astype(target.dtype)
+
+    def for_pair(i, carry):
+        choose(2 * i + 1 - core, pair_out, i)
+        return carry
+
+    def for_own(i, carry):
+        choose(2 * i + core, pair_own, i)
+        return carry
+
+    lax.fori_loop(0, chips, for_pair, 0)
+    pair = remote(pair_out, pair_in, pair_send, pair_recv, group=2 * chip + 1 - core)
+    pair.start()
+    lax.fori_loop(0, chips, for_own, 0)
+    pair.wait_recv()
+
+    def add_pair(to):
+        partial[to] = (pair_own[to] + pair_in[to].astype(jnp.float32)).astype(jnp.bfloat16)
+
+    def add_and_send(i):
+        add_pair(chip_peer(i))
 
         @pl.when(i > 1)
         def _():
-            sum_copy(group_peer(i - 1)).start()
-
-    each(groups, choose_and_send)
-    choose(mine)
-    sum_copy(group_peer(groups - 1)).start()
-    arrived[mine] = partial[mine]
-
-    other_parts = raw.at[pl.ds(0, parts - 1)]
-    remote(other_parts, other_parts, raw_send, raw_recv, group=mine).wait_recv()
+            sum_copy(chip_peer(i - 1)).start()
+
+    each(chips, add_and_send)
+    add_pair(chip)
+    sum_copy(chip_peer(chips - 1)).start()
+    arrived[chip] = partial[chip]
+
     total = jnp.zeros((seqs, LANES), jnp.float32)
     for c in range(blocks):
         value = raw[c // heads, c % heads]
@@ -350,14 +405,14 @@
         1.0 / (1.0 + jnp.exp(chosen[0] - chosen[1])),
     ]
 
-    other_sums = arrived.at[pl.ds(0, groups - 1)]
+    other_sums = arrived.at[pl.ds(0, chips - 1)]
     remote(other_sums, other_sums, sum_send, sum_recv, group=mine).wait_recv()
     units = []
     for k in range(2):
         sums = []
         for q in range(2):
             value = arrived[0, 2 * k + q].astype(jnp.float32)
-            for s in range(1, groups):
+            for s in range(1, chips):
                 value = value + arrived[s, 2 * k + q].astype(jnp.float32)
             sums.append(value * scale)
         silu = sums[0] / (1.0 + jnp.exp(-sums[0]))
@@ -370,14 +425,9 @@
     remote(others, others, stream_send, stream_recv, tensor=rank).wait_send()
     remote(other_routes, other_routes, route_send, route_recv, group=mine).wait_send()
     remote(other_parts, other_parts, raw_send, raw_recv, group=mine).wait_send()
+    pair.wait_send()
     remote(other_sums, other_sums, sum_send, sum_recv, group=mine).wait_send()
-    most = columns.at[pl.ds(0, groups - 1)]
     remote(most, most, column_send, column_recv, group=mine).wait_send()
-
-    @pl.when(jnp.logical_not(at_home))
-    def _():
-        one = columns.at[0]
-        remote(one, one, column_send, column_recv, group=mine).wait_send()
 
     most_cache = cache_out.at[pl.ds(0, (tensors - 1) * pairs)]
     remote(most_cache, most_cache, cache_send, cache_recv, tensor=rank).wait_send()
@@ -448,18 +498,21 @@
             pltpu.VMEM((seqs, ROWS, LANES), bf16),
             pltpu.VMEM((seqs * ROWS, LANES), f32),
             pltpu.VMEM((parts, heads, seqs, LANES), bf16),
-            pltpu.VMEM((heads, seqs, LANES), bf16),
+            pltpu.VMEM((parts * heads, seqs, LANES), bf16),
             pltpu.VMEM((seqs, cols), bf16),
             pltpu.VMEM((groups, own_cols // LANES, seqs, LANES), bf16),
             pltpu.VMEM((groups * seqs, own_cols), bf16),
             pltpu.VMEM((groups, 2, seqs, LANES), i32),
             pltpu.VMEM((experts, groups * seqs, hidden), f32),
             pltpu.VMEM((experts, groups * seqs, hidden), f32),
-            pltpu.VMEM((groups, 4, seqs, hidden), bf16),
-            pltpu.VMEM((groups, 4, seqs, hidden), bf16),
+            pltpu.VMEM((groups // 2, 4, seqs, hidden), bf16),
+            pltpu.VMEM((groups // 2, 4, seqs, hidden), bf16),
+            pltpu.VMEM((groups // 2, 4, seqs, hidden), f32),
+            pltpu.VMEM((groups // 2, 4, seqs, hidden), bf16),
+            pltpu.VMEM((groups // 2, 4, seqs, hidden), bf16),
             dma((10,)),
         ]
-        + [dma(())] * 13,
+        + [dma(())] * 15,
         compiler_params=pltpu.CompilerParams(
             collective_id=0, has_side_effects=True
         ),

time: 43.1 us -> 38.3 us (0.89)
  the two profiles are of different devices: /device:TPU:17 before, /device:TPU:1 now
where the time goes in v3:
time: 38.3 us; the launch traced here: 38.2 us
  Pallas kernels  37.6 us (98%)
  between operations  0.64 us (2%)
    pallas_call x1, Pallas kernels, body(): pl.pallas_call(functools.partial(kernel, (groups, tensors, span)), out_sh...  36.6 us
    pallas_call x1, Pallas kernels, body(): pl.pallas_call(write_out, out_shape=(jax.ShapeDtypeStruct(updated.shape,...  1.02 us

profile of v3, /device:TPU:1, one launch (start us, length us, event | category | flops | bytes accessed | tf_op | source)
XLA Modules:
  0.0 38.2 jit_solution(7213084888025558090)
XLA Ops:
  0.6 36.6 %shard_map.121 = (bf16[8,6144]{1,0:T(8,128)(2,1)S(1)}, bf16[8,2,256]{2,1,0:T(2,128)(2,1)S(1)}, bf16[64,32,256]{2,1,0:T(8,128)(2,1)S(1)}) custom-call(s32[8]{0:T(128)} %lengths_hbm.1, s32[2,8]{1,0:T(2,128)} %bitcast.6, bf16[2,1024,256]{2,1,0:T(8,128)(2,1)} %cache_hbm.1, bf16[8,48,128]{2,1,0:T(8,128)(2,1)} %queries_hbm.1, bf16[8,8,256]{2,1,0:T(8,128)(2,1)} %fresh_hbm.1, ...), custom_call_target="tpu_custom_call" | custom-call | tf_op jit(solution)/shard_map/pallas_call | solution.py:477
  37.2 1.0 %shard_map.122 = (bf16[8,6144]{1,0:T(8,128)(2,1)}, bf16[8,2,256]{2,1,0:T(2,128)(2,1)}, bf16[64,32,256]{2,1,0:T(8,128)(2,1)}) custom-call(bf16[8,6144]{1,0:T(8,128)(2,1)S(1)} %get-tuple-element.9.updated, bf16[8,2,256]{2,1,0:T(2,128)(2,1)S(1)} %get-tuple-element.10.hidden_units, bf16[64,32,256]{2,1,0:T(8,128)(2,1)S(1)} %get-tuple-element.11.cache), custom_call_target="tpu_custom_call" | custom-call | tf_op jit(solution)/shard_map/pallas_call | solution.py:531

commit v4 on v3

--- a/solution.py
+++ b/solution.py
@@ -67,8 +67,6 @@
     raw_recv,
     cache_send,
     cache_recv,
-    route_send,
-    route_recv,
     column_send,
     column_recv,
     pair_send,
@@ -96,6 +94,8 @@
     chip = mine // 2
     core = lax.rem(mine, 2)
     lower = mine < chips
+    batch = mine // chips
+    half = chips // 2
 
     def group_peer(i):
         return lax.rem(mine + i, groups)
@@ -144,15 +144,12 @@
     def raw_copy(to):
         return remote(raw.at[part], raw.at[part], raw_send, raw_recv, tensor=seq * parts + to)
 
-    def route_copy(to):
-        return remote(routes.at[mine], routes.at[mine], route_send, route_recv, group=to)
-
     def column_copy(to):
         return remote(
-            scaled.at[pl.ds(to * own_blocks, own_blocks)],
+            scaled.at[to],
             columns.at[mine],
             column_send,
-            column_recv,
+            column_recv.at[batch],
             group=to,
         )
 
@@ -255,10 +252,15 @@
         value = jnp.zeros((seqs, LANES), jnp.int32)
         for s in range(seqs):
             value = jnp.where(sublane == s, routing[k, s], value)
-        routes[mine, k] = value
+        routes[k] = value
+    lane = lax.broadcasted_iota(jnp.int32, (seqs, LANES), 1)
+    both = jnp.where(lane < LANES // 2, routes[0], routes[1])
+    for to in range(groups):
+        scaled[to, own_blocks] = both.astype(jnp.float32).astype(jnp.bfloat16)
 
     pl.semaphore_wait(barrier, tensors - 1 + jnp.where(lower, 0, chips))
-    each(seqs, lambda i: stream_copy(seq_peer(i)).start())
+    for i in sorted(range(1, seqs), key=lambda i: -min(i, seqs - i)):
+        stream_copy(seq_peer(i)).start()
 
     @pl.when(lower)
     def _():
@@ -287,7 +289,7 @@
     def scale_part(at):
         for c in range(heads):
             tile = raw[at, c].astype(jnp.float32)
-            scaled[at * heads + c] = (tile * gain[pl.ds(at * heads + c, 1), :]).astype(
+            scaled[at * pieces + c // own_blocks, c % own_blocks] = (tile * gain[pl.ds(at * heads + c, 1), :]).astype(
                 jnp.bfloat16
             )
 
@@ -310,7 +312,6 @@
     def _():
         pl.semaphore_wait(barrier, 1)
 
-    each(groups, lambda i: route_copy(group_peer(i)).start())
     def send_part(at):
         for piece in range(pieces):
             to = at * pieces + piece
@@ -320,65 +321,90 @@
                 column_copy(to).start()
 
     send_part(part)
+    own_columns = pltpu.make_async_copy(
+        scaled.at[mine], columns.at[mine], column_recv.at[batch]
+    )
     other_parts = raw.at[pl.ds(0, parts - 1)]
     remote(other_parts, other_parts, raw_send, raw_recv, group=mine).wait_recv()
     for i in range(1, parts):
         scale_part(part_peer(i))
     for i in range(1, parts):
         send_part(part_peer(i))
-    columns[mine] = scaled[pl.ds(mine * own_blocks, own_blocks)]
-
-    other_routes = routes.at[pl.ds(0, groups - 1)]
-    remote(other_routes, other_routes, route_send, route_recv, group=mine).wait_recv()
-    most = columns.at[pl.ds(0, groups - 1)]
-    remote(most, most, column_send, column_recv, group=mine).wait_recv()
-    for c in range(own_blocks):
-        tokens[:, c * LANES : (c + 1) * LANES] = (
-            columns[:, c].astype(jnp.float32).reshape(groups * seqs, LANES).astype(jnp.bfloat16)
-        )
-    for e in range(experts):
-        gate_all[e] = jnp.dot(tokens[...], gate_w[e], preferred_element_type=jnp.float32)
-        up_all[e] = jnp.dot(tokens[...], up_w[e], preferred_element_type=jnp.float32)
+    own_columns.start()
 
     def choose(to, target, at):
         rows = pl.ds(pl.multiple_of(to * seqs, seqs), seqs)
+        both = columns[to, own_blocks].astype(jnp.float32)
+        swapped = pltpu.roll(both, LANES // 2, 1)
         for k in range(2):
-            route = routes[to, k]
+            near, far = (both, swapped) if k == 0 else (swapped, both)
+            route = jnp.where(lane < LANES // 2, near, far)
             route = jnp.concatenate([route] * (hidden // LANES), axis=1)
             for q, source in enumerate((gate_all, up_all)):
                 value = source[0, rows, :]
                 for e in range(1, experts):
-                    value = jnp.where(route == e, source[e, rows, :], value)
+                    value = jnp.where(route == float(e), source[e, rows, :], value)
                 target[at, 2 * k + q] = value.astype(target.dtype)
 
-    def for_pair(i, carry):
-        choose(2 * i + 1 - core, pair_out, i)
-        return carry
-
-    def for_own(i, carry):
-        choose(2 * i + core, pair_own, i)
-        return carry
-
-    lax.fori_loop(0, chips, for_pair, 0)
-    pair = remote(pair_out, pair_in, pair_send, pair_recv, group=2 * chip + 1 - core)
-    pair.start()
-    lax.fori_loop(0, chips, for_own, 0)
-    pair.wait_recv()
-
-    def add_pair(to):
-        partial[to] = (pair_own[to] + pair_in[to].astype(jnp.float32)).astype(jnp.bfloat16)
-
-    def add_and_send(i):
-        add_pair(chip_peer(i))
-
-        @pl.when(i > 1)
-        def _():
-            sum_copy(chip_peer(i - 1)).start()
-
-    each(chips, add_and_send)
-    add_pair(chip)
-    sum_copy(chip_peer(chips - 1)).start()
-    arrived[chip] = partial[chip]
+    def pair_copy(b):
+        at = pl.ds(b * half, half)
+        return remote(
+            pair_out.at[at],
+            pair_in.at[at],
+            pair_send.at[b],
+            pair_recv.at[b],
+            group=2 * chip + 1 - core,
+        )
+
+    def expert_batch(b):
+        some = columns.at[pl.ds(b * chips, chips)]
+        remote(some, some, column_send, column_recv.at[b], group=mine).wait_recv()
+        rows = pl.ds(b * chips * seqs, chips * seqs)
+        for c in range(own_blocks):
+            tokens[rows, c * LANES : (c + 1) * LANES] = (
+                columns[pl.ds(b * chips, chips), c]
+                .astype(jnp.float32)
+                .reshape(chips * seqs, LANES)
+                .astype(jnp.bfloat16)
+            )
+        for e in range(experts):
+            gate_all[e, rows, :] = jnp.dot(
+                tokens[rows, :], gate_w[e], preferred_element_type=jnp.float32
+            )
+            up_all[e, rows, :] = jnp.dot(
+                tokens[rows, :], up_w[e], preferred_element_type=jnp.float32
+            )
+
+        def for_pair(i, carry):
+            choose(2 * i + 1 - core, pair_out, i)
+            return carry
+
+        def for_own(i, carry):
+            choose(2 * i + core, pair_own, i)
+            return carry
+
+        lax.fori_loop(b * half, (b + 1) * half, for_pair, 0)
+        pair_copy(b).start()
+        lax.fori_loop(b * half, (b + 1) * half, for_own, 0)
+        pair_copy(b).wait_recv()
+        first = jnp.where(chip // half == b, half // 2, 0)
+        order = [
+            b * half + lax.rem(chip + first + i, half)
+            for i in sorted(range(half), key=lambda i: min(i, half - i))
+        ]
+
+        def send_sum(to):
+            @pl.when(to != chip)
+            def _():
+                sum_copy(to).start()
+
+        for n, to in enumerate(order):
+            partial[to] = (pair_own[to] + pair_in[to].astype(jnp.float32)).astype(jnp.bfloat16)
+            if n:
+                send_sum(order[n - 1])
+        send_sum(order[-1])
+
+    expert_batch(0)
 
     total = jnp.zeros((seqs, LANES), jnp.float32)
     for c in range(blocks):
@@ -396,7 +422,7 @@
     expert_id = lax.broadcasted_iota(jnp.int32, (seqs, experts), 1)
     chosen = [
         jnp.sum(
-            jnp.where(routes[mine, k][:, :1] == expert_id, logits, 0.0), axis=1, keepdims=True
+            jnp.where(routes[k][:, :1] == expert_id, logits, 0.0), axis=1, keepdims=True
         )
         for k in range(2)
     ]
@@ -405,6 +431,8 @@
         1.0 / (1.0 + jnp.exp(chosen[0] - chosen[1])),
     ]
 
+    expert_batch(1)
+    arrived[chip] = partial[chip]
     other_sums = arrived.at[pl.ds(0, chips - 1)]
     remote(other_sums, other_sums, sum_send, sum_recv, group=mine).wait_recv()
     units = []
@@ -423,11 +451,12 @@
         )
 
     remote(others, others, stream_send, stream_recv, tensor=rank).wait_send()
-    remote(other_routes, other_routes, route_send, route_recv, group=mine).wait_send()
     remote(other_parts, other_parts, raw_send, raw_recv, group=mine).wait_send()
-    pair.wait_send()
+    for b in range(2):
+        pair_copy(b).wait_send()
     remote(other_sums, other_sums, sum_send, sum_recv, group=mine).wait_send()
-    remote(most, most, column_send, column_recv, group=mine).wait_send()
+    most = columns.at[pl.ds(0, groups - 1)]
+    remote(most, most, column_send, column_recv.at[0], group=mine).wait_send()
 
     most_cache = cache_out.at[pl.ds(0, (tensors - 1) * pairs)]
     remote(most_cache, most_cache, cache_send, cache_recv, tensor=rank).wait_send()
@@ -498,11 +527,11 @@
             pltpu.VMEM((seqs, ROWS, LANES), bf16),
             pltpu.VMEM((seqs * ROWS, LANES), f32),
             pltpu.VMEM((parts, heads, seqs, LANES), bf16),
-            pltpu.VMEM((parts * heads, seqs, LANES), bf16),
+            pltpu.VMEM((groups, own_cols // LANES + 1, seqs, LANES), bf16),
             pltpu.VMEM((seqs, cols), bf16),
-            pltpu.VMEM((groups, own_cols // LANES, seqs, LANES), bf16),
+            pltpu.VMEM((groups, own_cols // LANES + 1, seqs, LANES), bf16),
             pltpu.VMEM((groups * seqs, own_cols), bf16),
-            pltpu.VMEM((groups, 2, seqs, LANES), i32),
+            pltpu.VMEM((2, seqs, LANES), i32),
             pltpu.VMEM((experts, groups * seqs, hidden), f32),
             pltpu.VMEM((experts, groups * seqs, hidden), f32),
             pltpu.VMEM((groups // 2, 4, seqs, hidden), bf16),
@@ -512,7 +541,9 @@
             pltpu.VMEM((groups // 2, 4, seqs, hidden), bf16),
             dma((10,)),
         ]
-        + [dma(())] * 15,
+        + [dma(())] * 8
+        + [dma((2,))] * 3
+        + [dma(())] * 2,
         compiler_params=pltpu.CompilerParams(
             collective_id=0, has_side_effects=True
         ),

time: 38.3 us -> 36.1 us (0.943)
  Pallas kernels: 37.6 us -> 35.2 us
    pallas_call x1, Pallas kernels: 36.6 us -> 34.1 us  [body(): pl.pallas_call(functools.partial(kernel, (groups, tensors, span)), out_sh...]
where the time goes in v4:
time: 36.1 us; the launch traced here: 35.8 us
  Pallas kernels  35.2 us (98%)
  between operations  0.64 us (2%)
    pallas_call x1, Pallas kernels, body(): pl.pallas_call(functools.partial(kernel, (groups, tensors, span)), out_sh...  34.1 us
    pallas_call x1, Pallas kernels, body(): pl.pallas_call(write_out, out_shape=(jax.ShapeDtypeStruct(updated.shape,...  1.02 us

profile of v4, /device:TPU:1, one launch (start us, length us, event | category | flops | bytes accessed | tf_op | source)
XLA Modules:
  0.0 35.8 jit_solution(18285698865268579375)
XLA Ops:
  0.6 34.1 %shard_map.121 = (bf16[8,6144]{1,0:T(8,128)(2,1)S(1)}, bf16[8,2,256]{2,1,0:T(2,128)(2,1)S(1)}, bf16[64,32,256]{2,1,0:T(8,128)(2,1)S(1)}) custom-call(s32[8]{0:T(128)} %lengths_hbm.1, s32[2,8]{1,0:T(2,128)} %bitcast.6, bf16[2,1024,256]{2,1,0:T(8,128)(2,1)} %cache_hbm.1, bf16[8,48,128]{2,1,0:T(8,128)(2,1)} %queries_hbm.1, bf16[8,8,256]{2,1,0:T(8,128)(2,1)} %fresh_hbm.1, ...), custom_call_target="tpu_custom_call" | custom-call | tf_op jit(solution)/shard_map/pallas_call | solution.py:506
  34.8 1.0 %shard_map.122 = (bf16[8,6144]{1,0:T(8,128)(2,1)}, bf16[8,2,256]{2,1,0:T(2,128)(2,1)}, bf16[64,32,256]{2,1,0:T(8,128)(2,1)}) custom-call(bf16[8,6144]{1,0:T(8,128)(2,1)S(1)} %get-tuple-element.9.updated, bf16[8,2,256]{2,1,0:T(2,128)(2,1)S(1)} %get-tuple-element.10.hidden_units, bf16[64,32,256]{2,1,0:T(8,128)(2,1)S(1)} %get-tuple-element.11.cache), custom_call_target="tpu_custom_call" | custom-call | tf_op jit(solution)/shard_map/pallas_call | solution.py:562

commit v5 on v4

--- a/solution.py
+++ b/solution.py
@@ -14,8 +14,11 @@
 NT = (((1,), (1,)), ((), ()))
 
 
-def FIRST(down, along):
-    return along == 0
+EARLY = 2
+
+
+def goes_first(down, along):
+    return along == 0 or down in (0, 1, 7) or (down in (2, 6) and along == 2)
 
 
 def kernel(
@@ -94,8 +97,8 @@
     chip = mine // 2
     core = lax.rem(mine, 2)
     lower = mine < chips
-    batch = mine // chips
-    half = chips // 2
+    batches = ((0, EARLY), (EARLY, chips))
+    batch = jnp.where(chip < EARLY, 0, 1)
 
     def group_peer(i):
         return lax.rem(mine + i, groups)
@@ -279,7 +282,7 @@
     )
     keep.start()
     for offset in offsets:
-        if FIRST(*offset):
+        if goes_first(*offset):
             cache_copy(tensor_peer(*offset)).start()
     for load in loads[6:]:
         load.wait()
@@ -299,7 +302,7 @@
         raw[part, c] = stream_rows[pl.ds(c, seqs, stride=ROWS), :].astype(jnp.bfloat16)
     each(parts, lambda i: raw_copy(part_peer(i)).start())
     for offset in offsets:
-        if not FIRST(*offset):
+        if not goes_first(*offset):
             cache_copy(tensor_peer(*offset)).start()
     scale_part(part)
 
@@ -347,7 +350,8 @@
                 target[at, 2 * k + q] = value.astype(target.dtype)
 
     def pair_copy(b):
-        at = pl.ds(b * half, half)
+        first, last = batches[b]
+        at = pl.ds(first, last - first)
         return remote(
             pair_out.at[at],
             pair_in.at[at],
@@ -357,14 +361,16 @@
         )
 
     def expert_batch(b):
-        some = columns.at[pl.ds(b * chips, chips)]
+        first, last = batches[b]
+        count = last - first
+        some = columns.at[pl.ds(2 * first, 2 * count)]
         remote(some, some, column_send, column_recv.at[b], group=mine).wait_recv()
-        rows = pl.ds(b * chips * seqs, chips * seqs)
+        rows = pl.ds(2 * first * seqs, 2 * count * seqs)
         for c in range(own_blocks):
             tokens[rows, c * LANES : (c + 1) * LANES] = (
-                columns[pl.ds(b * chips, chips), c]
+                columns[pl.ds(2 * first, 2 * count), c]
                 .astype(jnp.float32)
-                .reshape(chips * seqs, LANES)
+                .reshape(2 * count * seqs, LANES)
                 .astype(jnp.bfloat16)
             )
         for e in range(experts):
@@ -383,15 +389,11 @@
             choose(2 * i + core, pair_own, i)
             return carry
 
-        lax.fori_loop(b * half, (b + 1) * half, for_pair, 0)
+        lax.fori_loop(first, last, for_pair, 0)
         pair_copy(b).start()
-        lax.fori_loop(b * half, (b + 1) * half, for_own, 0)
+        lax.fori_loop(first, last, for_own, 0)
         pair_copy(b).wait_recv()
-        first = jnp.where(chip // half == b, half // 2, 0)
-        order = [
-            b * half + lax.rem(chip + first + i, half)
-            for i in sorted(range(half), key=lambda i: min(i, half - i))
-        ]
+        order = list(range(first, last))
 
         def send_sum(to):
             @pl.when(to != chip)
@@ -523,7 +525,7 @@
             pltpu.VMEM((experts, cols), bf16),
             pltpu.VMEM(expert_gate.shape, bf16),
             pltpu.VMEM(expert_up.shape, bf16),
-            pltpu.VMEM((ROWS * seqs, LANES), f32),
+            pltpu.VMEM(((ROWS + 1) * seqs, LANES), f32),
             pltpu.VMEM((seqs, ROWS, LANES), bf16),
             pltpu.VMEM((seqs * ROWS, LANES), f32),
             pltpu.VMEM((parts, heads, seqs, LANES), bf16),

time: 36.1 us -> 35.7 us (0.989)
  the two profiles are of different devices: /device:TPU:1 before, /device:TPU:256 now
where the time goes in v5:
time: 35.7 us; the launch traced here: 35.6 us
  Pallas kernels  34.9 us (98%)
  between operations  0.64 us (2%)
    pallas_call x1, Pallas kernels, body(): pl.pallas_call(functools.partial(kernel, (groups, tensors, span)), out_sh...  33.9 us
    pallas_call x1, Pallas kernels, body(): pl.pallas_call(write_out, out_shape=(jax.ShapeDtypeStruct(updated.shape,...  1.02 us

profile of v5, /device:TPU:256, one launch (start us, length us, event | category | flops | bytes accessed | tf_op | source)
XLA Modules:
  0.0 35.6 jit_solution(17147940885821715814)
XLA Ops:
  0.6 33.9 %shard_map.121 = (bf16[8,6144]{1,0:T(8,128)(2,1)S(1)}, bf16[8,2,256]{2,1,0:T(2,128)(2,1)S(1)}, bf16[64,32,256]{2,1,0:T(8,128)(2,1)S(1)}) custom-call(s32[8]{0:T(128)} %lengths_hbm.1, s32[2,8]{1,0:T(2,128)} %bitcast.6, bf16[2,1024,256]{2,1,0:T(8,128)(2,1)} %cache_hbm.1, bf16[8,48,128]{2,1,0:T(8,128)(2,1)} %queries_hbm.1, bf16[8,8,256]{2,1,0:T(8,128)(2,1)} %fresh_hbm.1, ...), custom_call_target="tpu_custom_call" | custom-call | tf_op jit(solution)/shard_map/pallas_call | solution.py:508
  34.6 1.0 %shard_map.122 = (bf16[8,6144]{1,0:T(8,128)(2,1)}, bf16[8,2,256]{2,1,0:T(2,128)(2,1)}, bf16[64,32,256]{2,1,0:T(8,128)(2,1)}) custom-call(bf16[8,6144]{1,0:T(8,128)(2,1)S(1)} %get-tuple-element.9.updated, bf16[8,2,256]{2,1,0:T(2,128)(2,1)S(1)} %get-tuple-element.10.hidden_units, bf16[64,32,256]{2,1,0:T(8,128)(2,1)S(1)} %get-tuple-element.11.cache), custom_call_target="tpu_custom_call" | custom-call | tf_op jit(solution)/shard_map/pallas_call | solution.py:564

commit v6 on v5

--- a/solution.py
+++ b/solution.py
@@ -171,6 +171,10 @@
 
         lax.fori_loop(1, count, go, 0)
 
+    barrier = pltpu.get_barrier_semaphore()
+    for offset in offsets:
+        signal(tensor=tensor_peer(*offset))
+
     loads = [
         pltpu.make_async_copy(source, target, load_sem.at[k])
         for k, (source, target) in enumerate(
@@ -188,15 +192,13 @@
             )
         )
     ]
-    for load in loads:
+    for load in loads[:6]:
         load.start()
-
-    barrier = pltpu.get_barrier_semaphore()
-    for offset in offsets:
-        signal(tensor=tensor_peer(*offset))
 
     for load in loads[:6]:
         load.wait()
+    for load in loads[6:]:
+        load.start()
 
     length = lengths[seq]
     fresh_rows = fresh[...].astype(jnp.float32)

time: 35.7 us -> 35.7 us (level)
  the two profiles are of different devices: /device:TPU:256 before, /device:TPU:1 now
where the time goes in v6:
time: 35.7 us; the launch traced here: 35.5 us
  Pallas kernels  34.9 us (98%)
  between operations  0.64 us (2%)
    pallas_call x1, Pallas kernels, body(): pl.pallas_call(functools.partial(kernel, (groups, tensors, span)), out_sh...  33.9 us
    pallas_call x1, Pallas kernels, body(): pl.pallas_call(write_out, out_shape=(jax.ShapeDtypeStruct(updated.shape,...  1.02 us

profile of v6, /device:TPU:1, one launch (start us, length us, event | category | flops | bytes accessed | tf_op | source)
XLA Modules:
  0.0 35.5 jit_solution(4449272524244571288)
XLA Ops:
  0.6 33.9 %shard_map.121 = (bf16[8,6144]{1,0:T(8,128)(2,1)S(1)}, bf16[8,2,256]{2,1,0:T(2,128)(2,1)S(1)}, bf16[64,32,256]{2,1,0:T(8,128)(2,1)S(1)}) custom-call(s32[8]{0:T(128)} %lengths_hbm.1, s32[2,8]{1,0:T(2,128)} %bitcast.6, bf16[2,1024,256]{2,1,0:T(8,128)(2,1)} %cache_hbm.1, bf16[8,48,128]{2,1,0:T(8,128)(2,1)} %queries_hbm.1, bf16[8,8,256]{2,1,0:T(8,128)(2,1)} %fresh_hbm.1, ...), custom_call_target="tpu_custom_call" | custom-call | tf_op jit(solution)/shard_map/pallas_call | solution.py:510
  34.5 1.0 %shard_map.122 = (bf16[8,6144]{1,0:T(8,128)(2,1)}, bf16[8,2,256]{2,1,0:T(2,128)(2,1)}, bf16[64,32,256]{2,1,0:T(8,128)(2,1)}) custom-call(bf16[8,6144]{1,0:T(8,128)(2,1)S(1)} %get-tuple-element.9.updated, bf16[8,2,256]{2,1,0:T(2,128)(2,1)S(1)} %get-tuple-element.10.hidden_units, bf16[64,32,256]{2,1,0:T(8,128)(2,1)S(1)} %get-tuple-element.11.cache), custom_call_target="tpu_custom_call" | custom-call | tf_op jit(solution)/shard_map/pallas_call | solution.py:566

commit v7 on v6

--- a/solution.py
+++ b/solution.py
@@ -14,7 +14,7 @@
 NT = (((1,), (1,)), ((), ()))
 
 
-EARLY = 2
+EARLY = 3
 
 
 def goes_first(down, along):

time: 35.7 us -> 35.7 us (level)
  no operation moved by 1% of the time
where the time goes in v7:
time: 35.7 us; the launch traced here: 35.5 us
  Pallas kernels  34.9 us (98%)
  between operations  0.64 us (2%)
    pallas_call x1, Pallas kernels, body(): pl.pallas_call(functools.partial(kernel, (groups, tensors, span)), out_sh...  33.9 us
    pallas_call x1, Pallas kernels, body(): pl.pallas_call(write_out, out_shape=(jax.ShapeDtypeStruct(updated.shape,...  1.02 us

profile of v7, /device:TPU:1, one launch (start us, length us, event | category | flops | bytes accessed | tf_op | source)
XLA Modules:
  0.0 35.5 jit_solution(8606737120718069219)
XLA Ops:
  0.6 33.9 %shard_map.121 = (bf16[8,6144]{1,0:T(8,128)(2,1)S(1)}, bf16[8,2,256]{2,1,0:T(2,128)(2,1)S(1)}, bf16[64,32,256]{2,1,0:T(8,128)(2,1)S(1)}) custom-call(s32[8]{0:T(128)} %lengths_hbm.1, s32[2,8]{1,0:T(2,128)} %bitcast.6, bf16[2,1024,256]{2,1,0:T(8,128)(2,1)} %cache_hbm.1, bf16[8,48,128]{2,1,0:T(8,128)(2,1)} %queries_hbm.1, bf16[8,8,256]{2,1,0:T(8,128)(2,1)} %fresh_hbm.1, ...), custom_call_target="tpu_custom_call" | custom-call | tf_op jit(solution)/shard_map/pallas_call | solution.py:510
  34.5 1.0 %shard_map.122 = (bf16[8,6144]{1,0:T(8,128)(2,1)}, bf16[8,2,256]{2,1,0:T(2,128)(2,1)}, bf16[64,32,256]{2,1,0:T(8,128)(2,1)}) custom-call(bf16[8,6144]{1,0:T(8,128)(2,1)S(1)} %get-tuple-element.9.updated, bf16[8,2,256]{2,1,0:T(2,128)(2,1)S(1)} %get-tuple-element.10.hidden_units, bf16[64,32,256]{2,1,0:T(8,128)(2,1)S(1)} %get-tuple-element.11.cache), custom_call_target="tpu_custom_call" | custom-call | tf_op jit(solution)/shard_map/pallas_call | solution.py:566
